TPU v7x, 256 devices: a whole 4x4x8 slice. The times are simulated.
256 devices in a mesh: outer: 2 (over z_hi), dp: 8 (over z_lo, core), tensor: 16 (over x, y).
Axes of the slice: x: 4, y: 4, z: 8 (z_hi: 2, z_lo: 4; z = z_hi * 4 + z_lo), core: 2. Of those that a mesh axis runs over, the one named last changes fastest.
Arguments:
- attn: bfloat16 [4096, 8192], P(('outer', 'dp'), 'tensor'), may hold values from -6 to 6
- out_weight: bfloat16 [8192, 8192], P(None, 'tensor'), may hold values from -0.0625 to 0.0625
- resid: bfloat16 [4096, 8192], P(('outer', 'dp'), 'tensor'), may hold values from -8 to 8
- norm_gain: bfloat16 [8192], P('tensor'), may hold values from 0.5 to 1.5
- head: bfloat16 [8192], P('tensor'), may hold values from -1 to 1
- lengths: int32 [64], P(('outer', 'dp')), may hold values from 1 to 64
- pairs: int32 [64, 2], P(('outer', 'dp')), may hold values from 0 to 3, as said below
- pair_valid: int32 [64], P(('outer', 'dp')), may hold values from 0 to 1, as said below
- loss_scale: float32 [1], replicated, may hold values from 1024 to 8192
Outputs:
- loss: float32 [1], replicated
- grad_out_proj: float32 [8192, 8192], P(('outer', 'dp'), 'tensor')
- grad_gain: float32 [8192], P('tensor')
- grad_head: float32 [8192], P('tensor')
Inputs may be any that keep to these rules, and one draw needn't show every extreme that they name: `pairs`: in each pair the two numbers differ; the first pair of each replica is valid. `pair_valid`: the first of each replica's 4 entries is 1.
All inputs are finite; a program needn't handle non-finite values.
Results may differ from a plain program's by a relative error of at most 0.003.
Values may be sent and summed in bfloat16 or wider, within the bound.
A program may use at most 128 MiB of HBM per device.

v0:
```python
import jax
import jax.numpy as jnp
from jax import lax
from jax.sharding import Mesh
from jax.sharding import PartitionSpec as P

TENSOR = ("tensor_0", "tensor_1")


def one_axis_at_a_time(array, axes):
    for axis in axes:
        array = lax.psum(array, axis)
    return array


def copy_for_each(array, axis):
    copies = jnp.broadcast_to(array, (lax.axis_size(axis), *array.shape))
    return lax.all_to_all(copies, axis, split_axis=0, concat_axis=0, tiled=True)


def over_copies(array, axis):
    everything = copy_for_each(array, axis)
    return jnp.sum(everything, axis=0)


def packed_total(arrays, axis):
    ravelled, at, outs = (jnp.concatenate([a.reshape(-1) for a in arrays]), 0, [])
    subtotal = over_copies(ravelled, axis)
    for a in arrays:
        outs.append(subtotal[at : at + a.size].reshape(a.shape))
        at += a.size
    return tuple(outs)


def shards(attn, out_weight, resid, norm_gain, head, lengths, pairs, pair_valid, loss_scale):
    f32 = jnp.float32
    tok_dev = attn.shape[0]
    feats = resid.shape[1]
    width = feats * lax.axis_size(TENSOR)
    seqs_dev = lengths.shape[0]
    seq_len = tok_dev // seqs_dev
    valid = pair_valid.astype(f32)
    piece = out_weight
    proj = lax.psum_scatter(
        lax.dot_general(piece, attn, (((1,), (1,)), ((), ())), preferred_element_type=f32),
        TENSOR,
        scatter_dimension=0,
        tiled=True,
    )
    z = resid.astype(f32).T + proj
    gain = norm_gain.astype(f32)[:, None]
    headv = head.astype(f32)[:, None]
    squares = one_axis_at_a_time(jnp.sum(z * z, axis=0), TENSOR)
    inv = 1.0 / jnp.sqrt(squares / width + 1e-05)
    normed = z * inv[None, :] * gain
    partial_score = jnp.sum(normed * headv, axis=0)
    position = jnp.arange(tok_dev)
    seq_of = position // seq_len
    within = position % seq_len
    member = (within[:, None] < lengths[None, :]) & (
        seq_of[:, None] == jnp.arange(seqs_dev)[None, :]
    )
    pooling = member.astype(f32) / lengths.astype(f32)[None, :]
    score = one_axis_at_a_time(partial_score, TENSOR)
    reward = jnp.sum(pooling * score[:, None], axis=0)
    choose = jnp.arange(seqs_dev)[None, :]
    select = (pairs[:, 0:1] == choose).astype(f32) - (pairs[:, 1:2] == choose).astype(f32)
    margin = jnp.sum(select * reward[None, :], axis=1)
    loss_part = jnp.sum(valid * jax.nn.softplus(-margin))
    loss_sum, count = packed_total((loss_part, jnp.sum(valid)), ("outer", "dp"))
    dmargin = -loss_scale[0] * valid * jax.nn.sigmoid(-margin) / count
    dreward = jnp.sum(dmargin[:, None] * select, axis=0)
    dscore = jnp.sum(pooling * dreward[None, :], axis=1)
    head_part = jnp.sum(normed * dscore[None, :], axis=1)
    gain_part = jnp.sum(headv * z * (inv * dscore)[None, :], axis=1)
    scaled = dscore[None, :] * headv * gain
    inner = dscore * score / inv
    dproj = inv[None, :] * scaled - z * (inv**3 * inner / width)[None, :]
    dproj = dproj.astype(jnp.bfloat16)
    gathered = lax.all_gather(dproj, TENSOR, axis=0, tiled=True)
    piece = gathered
    grad_out_proj = lax.psum_scatter(
        jnp.dot(piece, attn, preferred_element_type=f32),
        ("outer", "dp"),
        scatter_dimension=0,
        tiled=True,
    )
    grad_gain, grad_head = packed_total((gain_part, head_part), ("outer", "dp"))
    loss = (loss_sum / count).reshape(1)
    return (loss, grad_out_proj, grad_gain, grad_head)


def solution(mesh):
    finer = Mesh(
        mesh.devices.reshape(mesh.shape["outer"], mesh.shape["dp"], 4, 4),
        ("outer", "dp", "tensor_0", "tensor_1"),
    )
    placed = (
        P(("outer", "dp"), TENSOR),
        P(None, TENSOR),
        P(("outer", "dp"), TENSOR),
        P(TENSOR),
        P(TENSOR),
        P(("outer", "dp")),
        P(("outer", "dp"), None),
        P(("outer", "dp")),
        P(),
    )
    return jax.shard_map(
        shards,
        mesh=finer,
        in_specs=placed,
        out_specs=(P(), P(("outer", "dp"), TENSOR), P(TENSOR), P(TENSOR)),
        check_vma=False,
    )
```

profile of v0, /device:TPU:4, one launch (start us, length us, event | category | flops | bytes accessed | tf_op | source)
XLA Modules:
  0.0 338.1 jit_solution(8251019488266016324)
XLA Ops:
  7.2 0.0 copy-start
  7.2 0.0 reduce-scatter.3.cloned.1.call-start
  7.2 0.9 copy-done
  8.1 9.0 %fusion.10 = f32[8192,256]{1,0:T(8,128)} fusion(bf16[8192,512]{1,0:T(8,128)(2,1)} %param.10, bf16[256,512]{1,0:T(8,128)(2,1)S(1)} %copy-done), kind=kOutput, calls=%fused_computation.40 | convolution fusion | flops 2147483648 | bytes 17039360 | tf_op jit(solution)/shard_map/dot_general | solution.py:45
  17.1 0.0 copy-start.2
  17.1 0.0 copy-start.4
  17.1 0.0 copy-start.5
  17.1 0.0 copy-start.6
  17.1 0.0 copy-start.3
  17.1 0.0 reduce-scatter.3.cloned.1.call-update
  17.2 0.6 copy-done.2
  17.8 0.0 copy-done.4
  17.8 0.0 copy-done.5
  17.8 0.3 copy-done.1
  18.1 0.1 copy.15
  18.3 0.0 copy-done.6
  18.3 92.4 %reduce-scatter.3.cloned.1.call-done = f32[512,256]{1,0:T(8,128)} async-done(((f32[8192,256]{1,0:T(8,128)}), f32[512,256]{1,0:T(8,128)}) %reduce-scatter.3.cloned.1.call-update) | async-done | bytes 524304 | tf_op jit(solution)/shard_map/reduce_scatter | solution.py:44
  110.6 1.1 multiply_reduce_fusion.3
  111.8 8.4 %psum.28 = f32[256]{0:T(256)S(1)} all-reduce(f32[256]{0:T(256)S(1)} %multiply_reduce_fusion.3), channel_id=1, replica_groups=mesh['outer'=2,'dp'=8,'tensor_0'=4,'tensor_1'=4] {'tensor_0'}, use_global_device_ids=true, to_apply=%region_2.0 | all-reduce | flops 256 | bytes 2048 | tf_op jit(solution)/shard_map/psum | solution.py:12
  120.1 8.5 %psum.29 = f32[256]{0:T(256)S(1)} all-reduce(f32[256]{0:T(256)S(1)} %psum.28), channel_id=1, replica_groups=mesh['outer'=2,'dp'=8,'tensor_0'=4,'tensor_1'=4] {'tensor_1'}, use_global_device_ids=true, to_apply=%region_3.0 | all-reduce | flops 256 | bytes 2048 | tf_op jit(solution)/shard_map/psum | solution.py:12
  128.6 1.3 multiply_reduce_fusion.2
  129.9 9.0 %psum.30 = f32[256]{0:T(256)S(1)} all-reduce(f32[256]{0:T(256)S(1)} %multiply_reduce_fusion.2), channel_id=1, replica_groups=mesh['outer'=2,'dp'=8,'tensor_0'=4,'tensor_1'=4] {'tensor_0'}, use_global_device_ids=true, to_apply=%region_5.6 | all-reduce | flops 256 | bytes 2048 | tf_op jit(solution)/shard_map/psum | solution.py:12
  138.9 8.0 %psum.31 = f32[256]{0:T(256)S(1)} all-reduce(f32[256]{0:T(256)S(1)} %psum.30), channel_id=1, replica_groups=mesh['outer'=2,'dp'=8,'tensor_0'=4,'tensor_1'=4] {'tensor_1'}, use_global_device_ids=true, to_apply=%region_6.7 | all-reduce | flops 256 | bytes 2048 | tf_op jit(solution)/shard_map/psum | solution.py:12
  146.9 0.2 multiply_reduce_fusion.5
  147.1 0.2 multiply_reduce_fusion.7
  147.3 0.0 copy-done.3
  147.3 0.6 fusion.5
  147.9 1.4 pad_maximum_fusion.1
  149.3 0.6 broadcast_in_dim.4
  149.9 7.1 %all-to-all-start = ((f32[16,1,2]{2,1,0:T(1,128)}), f32[16,1,2]{2,1,0:T(1,128)S(1)}, u32[]{:S(2)}, u32[]{:S(2)}) async-start(f32[16,1,2]{2,1,0:T(1,128)} %broadcast_in_dim.4), calls=%async_computation.1 | async-start | bytes 16384 | tf_op jit(solution)/shard_map/all_to_all | solution.py:18
  157.0 0.0 all-gather.2.cloned.1.call-start
  157.7 6.8 %all-to-all-done = f32[16,1,2]{2,1,0:T(1,128)S(1)} async-done(((f32[16,1,2]{2,1,0:T(1,128)}), f32[16,1,2]{2,1,0:T(1,128)S(1)}, u32[]{:S(2)}, u32[]{:S(2)}) %all-to-all-start) | async-done | bytes 160 | tf_op jit(solution)/shard_map/all_to_all | solution.py:18
  164.6 0.6 fusion.9
  165.2 0.7 fusion.6
  165.9 0.1 multiply_reduce_fusion.6
  165.9 0.1 multiply_reduce_fusion.4
  166.1 2.0 multiply_reduce_fusion.1
  168.1 0.0 all-gather.2.cloned.1.call-update
  168.1 0.0 reduce-scatter.5.cloned.1.call-start
  168.2 51.4 %all-gather.2.cloned.1.call-done = bf16[8192,256]{1,0:T(8,128)(2,1)} async-done(((bf16[512,256]{1,0:T(8,128)(2,1)}), bf16[8192,256]{1,0:T(8,128)(2,1)}) %all-gather.2.cloned.1.call-update) | async-done | bytes 4194320 | tf_op jit(solution)/shard_map/all_gather | solution.py:80
  219.5 10.2 %fusion.11 = f32[8192,512]{1,0:T(8,128)} fusion(bf16[8192,256]{1,0:T(8,128)(2,1)} %all-gather.2.cloned.1.call-done, bf16[256,512]{1,0:T(8,128)(2,1)S(1)} %copy-done), kind=kOutput, calls=%fused_computation.41 | convolution fusion | flops 2147483648 | bytes 21233664 | tf_op jit(solution)/shard_map/dot_general | solution.py:83
  229.8 0.0 reduce-scatter.5.cloned.1.call-update
  229.8 0.7 broadcast_in_dim.5
  230.5 7.1 %all-to-all-start.1 = ((f32[16,1,1024]{2,1,0:T(1,128)}), f32[16,1,1024]{2,1,0:T(1,128)S(1)}, u32[]{:S(2)}, u32[]{:S(2)}) async-start(f32[16,1,1024]{2,1,0:T(1,128)} %broadcast_in_dim.5), calls=%async_computation.3 | async-start | bytes 131072 | tf_op jit(solution)/shard_map/all_to_all | solution.py:18
  238.9 6.5 %all-to-all-done.1 = f32[16,1,1024]{2,1,0:T(1,128)S(1)} async-done(((f32[16,1,1024]{2,1,0:T(1,128)}), f32[16,1,1024]{2,1,0:T(1,128)S(1)}, u32[]{:S(2)}, u32[]{:S(2)}) %all-to-all-start.1) | async-done | bytes 65568 | tf_op jit(solution)/shard_map/all_to_all | solution.py:18
  245.4 0.1 reduce_sum.119
  245.4 0.6 fusion.8
  246.0 84.4 %reduce-scatter.5.cloned.1.call-done = f32[512,512]{1,0:T(8,128)} async-done(((f32[8192,512]{1,0:T(8,128)}), f32[512,512]{1,0:T(8,128)}) %reduce-scatter.5.cloned.1.call-update) | async-done | bytes 1048592 | tf_op jit(solution)/shard_map/reduce_scatter | solution.py:82
  (10 shorter events, 0.1 us)
Async XLA Ops:
  7.2 1.0 copy-start
  7.2 103.4 %reduce-scatter.3.cloned.1.call-start = ((), (), s32[]{:S(2)}) async-start(), calls=%async_computation.4 | async-start | bytes 8912896 | tf_op jit(solution)/shard_map/reduce_scatter | solution.py:44
  17.1 0.7 copy-start.2
  17.1 0.7 copy-start.4
  17.1 0.7 copy-start.5
  17.1 1.0 copy-start.1
  17.1 1.1 copy-start.6
  17.1 130.2 %copy-start.3 = (s32[4]{0:T(128)S(1)}, s32[4]{0:T(128)}, u32[]{:S(2)}) copy-start(s32[4]{0:T(128)} %param.16) | copy-start | bytes 52
  149.9 14.7 %all-to-all-start = ((f32[16,1,2]{2,1,0:T(1,128)}), f32[16,1,2]{2,1,0:T(1,128)S(1)}, u32[]{:S(2)}, u32[]{:S(2)}) async-start(f32[16,1,2]{2,1,0:T(1,128)} %broadcast_in_dim.4), calls=%async_computation.1 | async-start | bytes 16384 | tf_op jit(solution)/shard_map/all_to_all | solution.py:18
  157.0 62.5 %all-gather.2.cloned.1.call-start = ((), (), s32[]{:S(2)}) async-start(), calls=%async_computation.5 | async-start | bytes 4456448 | tf_op jit(solution)/shard_map/all_gather | solution.py:80
  168.1 162.3 %reduce-scatter.5.cloned.1.call-start = ((), (), s32[]{:S(2)}) async-start(), calls=%async_computation.6 | async-start | bytes 17825792 | tf_op jit(solution)/shard_map/reduce_scatter | solution.py:82
  230.5 14.9 %all-to-all-start.1 = ((f32[16,1,1024]{2,1,0:T(1,128)}), f32[16,1,1024]{2,1,0:T(1,128)S(1)}, u32[]{:S(2)}, u32[]{:S(2)}) async-start(f32[16,1,1024]{2,1,0:T(1,128)} %broadcast_in_dim.5), calls=%async_computation.3 | async-start | bytes 131072 | tf_op jit(solution)/shard_map/all_to_all | solution.py:18
Sparse Core Ops, SparseCore 0:
  17.3 93.2 reduce-scatter.2
  168.2 51.2 all-gather.1
  229.9 100.4 reduce-scatter.4
where the time goes:
time: 339 us; the launch traced here: 338 us
  waiting for transfers between devices  241 us (71%)
  blocking collectives  33.9 us (10%)
  matrix products  19.2 us (6%)
  between operations  17 us (5%)
  starting transfers between devices  14.4 us (4%)
  other arithmetic  7.79 us (2%)
  local copies, waits for them, and re-layouts  4.42 us (1%)
    reduce_scatter x1, waiting for transfers between devices, shards(): lax.psum_scatter(lax.dot_general(piece, attn, (((1,), (1,)), ((), ())), p...  92.4 us
    reduce_scatter x1, waiting for transfers between devices, shards(): lax.psum_scatter(jnp.dot(piece, attn, preferred_element_type=f32), ('oute...  84.4 us
    all_gather x1, waiting for transfers between devices, shards(): gathered = lax.all_gather(dproj, TENSOR, axis=0, tiled=True)  51.4 us
    psum x4, blocking collectives, one_axis_at_a_time(): array = lax.psum(array, axis)  33.9 us
    all_to_all x2, starting transfers between devices, copy_for_each(): return lax.all_to_all(copies, axis, split_axis=0, concat_axis=0, tiled=True)  14.2 us
    all_to_all x2, waiting for transfers between devices, copy_for_each(): return lax.all_to_all(copies, axis, split_axis=0, concat_axis=0, tiled=True)  13.3 us
    dot_general x1, matrix products, shards(): jnp.dot(piece, attn, preferred_element_type=f32)  10.2 us
    dot_general x1, matrix products, shards(): lax.dot_general(piece, attn, (((1,), (1,)), ((), ())), preferred_element_...  8.98 us
  transfers between devices with their start and end apart: 5, of which 5 were waited for; matrix products, arithmetic and copies ran while one was open for 0% of the time, Pallas kernels for 0%

commit v1 on v0

v1 whole, which is shorter than its diff:
```python
import jax
import jax.numpy as jnp
from jax import lax
from jax.sharding import PartitionSpec as P

REP = ("outer", "dp")


def shards(attn, out_weight, resid, norm_gain, head, lengths, pairs, pair_valid, loss_scale):
    f32 = jnp.float32
    bf16 = jnp.bfloat16
    reps = 16
    cols = 16
    tok = attn.shape[0]
    part = tok // cols
    hd = attn.shape[1]
    feats = out_weight.shape[0] // reps
    width = out_weight.shape[0]
    seqs = lengths.shape[0]
    seq_len = tok // seqs
    r = lax.axis_index(REP)
    t = lax.axis_index("tensor")
    attn_all = lax.all_gather(attn, REP, axis=0, tiled=True)
    vec = jnp.stack([norm_gain, head])
    vec_all = lax.all_gather(vec, "tensor", axis=1, tiled=True)
    vec_r = lax.dynamic_slice(vec_all, (0, r * feats), (2, feats)).astype(f32)
    gain, headv = vec_r[0], vec_r[1]
    small = jnp.concatenate([lengths, pairs[:, 0], pairs[:, 1], pair_valid])
    small = lax.all_gather(small, REP, axis=0)
    lens_all, first, second, valid = (small[:, i * seqs : (i + 1) * seqs] for i in range(4))
    res = lax.all_to_all(resid, "tensor", split_axis=0, concat_axis=0, tiled=True)
    res = lax.all_to_all(res, REP, split_axis=0, concat_axis=0, tiled=True)
    w = lax.dynamic_slice(out_weight, (r * feats, 0), (feats, hd))
    part_sum = lax.dot_general(attn_all, w, (((1,), (1,)), ((), ())), preferred_element_type=f32)
    part_sum = part_sum.astype(bf16).reshape(reps, cols, part, feats).transpose(1, 0, 2, 3)
    part_sum = part_sum.reshape(cols * reps * part, feats)
    proj = lax.psum_scatter(part_sum, "tensor", scatter_dimension=0, tiled=True)
    z = res.astype(f32) + proj.astype(f32)
    stats = jnp.stack([jnp.sum(z * z, axis=1), jnp.sum(z * (gain * headv)[None, :], axis=1)])
    stats = lax.psum(stats, REP)
    inv = 1.0 / jnp.sqrt(stats[0] / width + 1e-05)
    score = inv * stats[1]
    per_seq = seq_len // part
    slot = (t % per_seq) * part + jnp.arange(part)
    seq = t // per_seq
    lens_mine = lens_all[:, seq]
    live = (slot[None, :] < lens_mine[:, None]).astype(f32)
    pool = jnp.sum(score.reshape(reps, part) * live, axis=1)
    onehot = (jnp.arange(seqs) == seq).astype(f32)
    rewards = lax.psum(pool[:, None] * onehot[None, :], "tensor") / lens_all.astype(f32)
    choose = jnp.arange(seqs)[None, None, :]
    select = (first[:, :, None] == choose).astype(f32) - (second[:, :, None] == choose).astype(f32)
    margin = jnp.sum(select * rewards[:, None, :], axis=2)
    vf = valid.astype(f32)
    count = jnp.sum(vf)
    loss = (jnp.sum(vf * jax.nn.softplus(-margin)) / count).reshape(1)
    dmargin = -loss_scale[0] * vf * jax.nn.sigmoid(-margin) / count
    dreward = jnp.sum(dmargin[:, :, None] * select, axis=1) / lens_all.astype(f32)
    dmine = dreward[:, seq]
    dscore = (live * dmine[:, None]).reshape(-1)
    k = inv * dscore
    c = inv * inv * dscore * score / width
    g = jnp.sum(k[:, None] * z, axis=0)
    dproj = (k[:, None] * (gain * headv)[None, :] - z * c[:, None]).astype(bf16)
    d_all = lax.all_gather(dproj, "tensor", axis=0, tiled=False)
    d_all = d_all.reshape(cols, reps, part, feats).transpose(1, 0, 2, 3).reshape(reps * tok, feats)
    out = lax.dot_general(d_all, attn_all, (((0,), (0,)), ((), ())), preferred_element_type=f32)
    g = lax.psum(g, "tensor")
    g = lax.all_gather(g, REP, axis=0)
    g = lax.dynamic_slice(g, (t, 0), (1, feats))[0]
    return (loss, out, g * head.astype(f32), g * norm_gain.astype(f32))


def solution(mesh):
    placed = (
        P(REP, "tensor"),
        P(None, "tensor"),
        P(REP, "tensor"),
        P("tensor"),
        P("tensor"),
        P(REP),
        P(REP, None),
        P(REP),
        P(),
    )
    return jax.shard_map(
        shards,
        mesh=mesh,
        in_specs=placed,
        out_specs=(P(), P(REP, "tensor"), P("tensor"), P("tensor")),
        check_vma=False,
    )
```

time: 339 us -> 291 us (0.86)
  waiting for transfers between devices: 241 us -> 89.7 us
  blocking collectives: 33.9 us -> 138 us
  local copies, waits for them, and re-layouts: 4.42 us -> 16 us
  matrix products: 19.2 us -> 10 us
    reduce_scatter x2 -> x1, waiting for transfers between devices: 177 us -> 31.4 us  [shards(): proj = lax.psum_scatter(part_sum, 'tensor', scatter_dimension=0, tiled=True)]
    psum x4 -> x3, blocking collectives: 33.9 us -> 88.1 us  [the longest x1 32.8 us: shards(): lax.psum(pool[:, None] * onehot[None, :], 'tensor') / lens_all.astype(f32)]
    all_gather x0 -> x2, blocking collectives: none -> 37.2 us  [the longest x1 23 us: shards(): vec_all = lax.all_gather(vec, 'tensor', axis=1, tiled=True)]
    all_to_all x2, waiting for transfers between devices: 13.3 us -> 0.01 us  [the longest x1 0.01 us: shards(): lax.all_to_all(resid, 'tensor', split_axis=0, concat_axis=0, tiled=True)]
    unnamed x0 -> x1, blocking collectives: none -> 12.5 us
    dot_general x2, matrix products: 19.2 us -> 10 us  [the longest x1 6.7 us: shards(): lax.dot_general(attn_all, w, (((1,), (1,)), ((), ())), preferred_element_...]
    convert_element_type x0 -> x1, local copies, waits for them, and re-layouts: none -> 6.52 us  [shards(): part_sum.astype(bf16).reshape(reps, cols, part, feats).transpose(1, 0, 2, 3)]
    all_gather x1 -> x2, waiting for transfers between devices: 51.4 us -> 57.6 us  [the longest x1 46.7 us: shards(): attn_all = lax.all_gather(attn, REP, axis=0, tiled=True)]
  transfers between devices with their start and end apart: 5 -> 5, of which waited for: 5 -> 3; matrix products, arithmetic and copies ran while one was open for 0% -> 1% of each run, Pallas kernels for 0% -> 0%
where the time goes in v1:
time: 291 us; the launch traced here: 289 us
  blocking collectives  138 us (47%)
  waiting for transfers between devices  89.7 us (31%)
  between operations  17.8 us (6%)
  local copies, waits for them, and re-layouts  16 us (5%)
  starting transfers between devices  12.4 us (4%)
  matrix products  10 us (3%)
  other arithmetic  5.51 us (2%)
    all_gather x1, waiting for transfers between devices, shards(): attn_all = lax.all_gather(attn, REP, axis=0, tiled=True)  46.7 us
    psum x1, blocking collectives, shards(): lax.psum(pool[:, None] * onehot[None, :], 'tensor') / lens_all.astype(f32)  32.8 us
    psum x1, blocking collectives, shards(): g = lax.psum(g, 'tensor')  31.5 us
    reduce_scatter x1, waiting for transfers between devices, shards(): proj = lax.psum_scatter(part_sum, 'tensor', scatter_dimension=0, tiled=True)  31.4 us
    psum x1, blocking collectives, shards(): stats = lax.psum(stats, REP)  23.9 us
    all_gather x1, blocking collectives, shards(): vec_all = lax.all_gather(vec, 'tensor', axis=1, tiled=True)  23 us
    all_gather x1, blocking collectives, shards(): g = lax.all_gather(g, REP, axis=0)  14.2 us
    unnamed x1, blocking collectives  12.5 us
  transfers between devices with their start and end apart: 5, of which 3 were waited for; matrix products, arithmetic and copies ran while one was open for 1% of the time, Pallas kernels for 0%

profile of v1, /device:TPU:4, one launch (start us, length us, event | category | flops | bytes accessed | tf_op | source)
XLA Modules:
  0.0 289.2 jit_solution(13689522608427997237)
XLA Ops:
  7.2 0.0 all-gather.6.cloned.1.call-start
  7.2 0.7 all-gather.6.cloned.1.call-update
  7.9 0.0 reduce-scatter.2.cloned.1.call-start
  8.0 46.7 %all-gather.6.cloned.1.call-done = bf16[4096,512]{1,0:T(8,128)(2,1)} async-done(((bf16[256,512]{1,0:T(8,128)(2,1)}), bf16[4096,512]{1,0:T(8,128)(2,1)}) %all-gather.6.cloned.1.call-update) | async-done | bytes 4194320 | tf_op jit(solution)/shard_map/all_gather | solution.py:23
  54.6 6.7 %fusion = bf16[4096,512]{0,1:T(8,128)(2,1)} fusion(bf16[4096,512]{1,0:T(8,128)(2,1)} %all-gather.6.cloned.1.call-done, bf16[8192,512]{1,0:T(8,128)(2,1)} %param.10, s32[]{:T(128)S(6)} %select_n.29), kind=kOutput, calls=%fused_computation.1 | convolution fusion | flops 2149580800 | bytes 8912900 | tf_op jit(solution)/shard_map/dot_general | solution.py:34
  61.3 6.5 %copy.30 = bf16[4096,512]{1,0:T(8,128)(2,1)} copy(bf16[4096,512]{0,1:T(8,128)(2,1)} %fusion) | data formatting | bytes 8388608 | tf_op jit(solution)/shard_map/convert_element_type | solution.py:35
  67.9 4.8 %copy.31 = bf16[16,16,16,512]{3,2,1,0:T(8,128)(2,1)} copy(bf16[16,16,16,512]{3,2,0,1:T(8,128)(2,1)} %bitcast.41) | data formatting | bytes 8388608 | tf_op jit(solution)/shard_map/transpose | solution.py:35
  72.7 0.0 copy-start.4
  72.7 0.0 copy-start.5
  72.7 0.0 reduce-scatter.2.cloned.1.call-update
  72.7 7.4 %all-to-all-start = ((bf16[16,16,512]{2,1,0:T(8,128)(2,1)}), bf16[16,16,512]{2,1,0:T(8,128)(2,1)}, u32[]{:S(2)}, u32[]{:S(2)}) async-start(bf16[16,16,512]{2,1,0:T(8,128)(2,1)} %bitcast.4), calls=%async_computation | async-start | bytes 524288 | tf_op jit(solution)/shard_map/all_to_all | solution.py:31
  80.1 0.0 copy-done.2
  80.2 0.0 copy-done.1
  80.2 0.0 copy-done.6
  80.2 0.6 dynamic-slice
  81.5 0.2 add_dynamic-update-slice_fusion
  81.7 12.5 %all-reduce = s32[256]{0:T(256)S(1)} all-reduce(s32[256]{0:T(256)S(1)} %add_dynamic-update-slice_fusion), channel_id=2, replica_groups=mesh['outer'=2,'dp'=8,'tensor'=16] {'outer','dp'}, use_global_device_ids=true, to_apply=%add | all-reduce | flops 256 | bytes 2048
  94.2 0.1 reshape.123
  94.3 0.1 fusion.12
  94.3 0.0 all-to-all-done
  94.3 4.8 %all-to-all-start.1 = ((bf16[16,16,512]{2,1,0:T(8,128)(2,1)}), bf16[16,16,512]{2,1,0:T(8,128)(2,1)S(1)}, u32[]{:S(2)}, u32[]{:S(2)}) async-start(bf16[16,16,512]{2,1,0:T(8,128)(2,1)} %all-to-all-done), calls=%async_computation.1 | async-start | bytes 524288 | tf_op jit(solution)/shard_map/all_to_all | solution.py:32
  99.2 0.0 all-gather.8.cloned.1.call-start
  99.2 0.1 copy.34
  99.3 0.1 copy.27
  99.4 0.1 copy.28
  99.5 0.1 copy.33
  100.2 23.0 %all_gather.27 = bf16[2,8192]{1,0:T(2,128)(2,1)S(1)} all-gather(bf16[2,512]{1,0:T(2,128)(2,1)S(1)} %pad_maximum_fusion), channel_id=1, replica_groups=mesh['outer'=2,'dp'=8,'tensor'=16] {'tensor'}, dimensions={1}, use_global_device_ids=true | all-gather | bytes 34816 | tf_op jit(solution)/shard_map/all_gather | solution.py:25
  123.3 0.0 all-to-all-done.1
  123.3 31.4 %reduce-scatter.2.cloned.1.call-done = bf16[256,512]{1,0:T(8,128)(2,1)} async-done(((bf16[4096,512]{1,0:T(8,128)(2,1)}), bf16[256,512]{1,0:T(8,128)(2,1)}) %reduce-scatter.2.cloned.1.call-update) | async-done | bytes 262160 | tf_op jit(solution)/shard_map/reduce_scatter | solution.py:37
  154.6 1.1 multiply_reduce_fusion.2
  155.8 23.9 %psum.21 = f32[2,256]{1,0:T(2,128)S(1)} all-reduce(f32[2,256]{1,0:T(2,128)S(1)} %pad_maximum_fusion.1), channel_id=1, replica_groups=mesh['outer'=2,'dp'=8,'tensor'=16] {'outer','dp'}, use_global_device_ids=true, to_apply=%region_3.0 | all-reduce | flops 512 | bytes 4096 | tf_op jit(solution)/shard_map/psum | solution.py:40
  179.7 0.1 mul.169
  179.8 0.2 fusion.2
  180.0 0.1 broadcast_multiply_fusion
  180.1 32.8 %psum.22 = f32[16,4]{0,1:T(4,128)S(1)} all-reduce(f32[16,4]{0,1:T(4,128)S(1)} %broadcast_multiply_fusion), channel_id=1, replica_groups=mesh['outer'=2,'dp'=8,'tensor'=16] {'tensor'}, use_global_device_ids=true, to_apply=%region_5.6 | all-reduce | flops 64 | bytes 512 | tf_op jit(solution)/shard_map/psum | solution.py:50
  212.9 0.6 convert_reduce_fusion
  213.5 0.7 fusion.5
  214.2 0.1 compare_select_fusion
  214.3 0.1 mul.185
  214.4 1.9 multiply_reduce_fusion
  216.2 0.0 all-gather.8.cloned.1.call-update
  217.6 31.5 %psum.23 = f32[1,512]{1,0:T(1,128)S(1)} all-reduce(f32[1,512]{1,0:T(1,128)S(1)} %bitcast.45), channel_id=1, replica_groups=mesh['outer'=2,'dp'=8,'tensor'=16] {'tensor'}, use_global_device_ids=true, to_apply=%region_11.12 | all-reduce | flops 512 | bytes 4096 | tf_op jit(solution)/shard_map/psum | solution.py:68
  249.0 14.2 %all-gather.2 = f32[16,1,512]{2,1,0:T(1,128)S(1)} all-gather(f32[1,1,512]{2,1,0:T(1,128)S(1)} %bitcast.46), channel_id=1, replica_groups=mesh['outer'=2,'dp'=8,'tensor'=16] {'outer','dp'}, dimensions={0}, use_global_device_ids=true | all-gather | bytes 34816 | tf_op jit(solution)/shard_map/all_gather | solution.py:69
  263.3 0.6 convert_multiply_fusion
  263.9 10.9 %all-gather.8.cloned.1.call-done = bf16[4096,512]{1,0:T(8,128)(2,1)} async-done(((bf16[256,512]{1,0:T(8,128)(2,1)}), bf16[4096,512]{1,0:T(8,128)(2,1)}) %all-gather.8.cloned.1.call-update) | async-done | bytes 4194320 | tf_op jit(solution)/shard_map/all_gather | solution.py:65
  274.7 2.8 copy.32
  277.6 0.6 copy-done
  278.2 3.3 %fusion.14 = f32[512,512]{1,0:T(8,128)} fusion(bf16[4096,512]{1,0:T(8,128)(2,1)S(1)} %bitcast.39, bf16[4096,512]{1,0:T(8,128)(2,1)S(1)} %copy-done), kind=kOutput, calls=%fused_computation.49 | convolution fusion | flops 2147483648 | bytes 9437184 | tf_op jit(solution)/shard_map/dot_general | solution.py:67
  (27 shorter events, 0.2 us)
Async XLA Ops:
  7.2 47.5 %all-gather.6.cloned.1.call-start = ((), (), s32[]{:S(2)}) async-start(), calls=%async_computation.3 | async-start | bytes 4456448 | tf_op jit(solution)/shard_map/all_gather | solution.py:23
  7.9 146.7 %reduce-scatter.2.cloned.1.call-start = ((), (), s32[]{:S(2)}) async-start(), calls=%async_computation.4 | async-start | bytes 4456448 | tf_op jit(solution)/shard_map/reduce_scatter | solution.py:37
  72.7 7.5 %copy-start.2 = (bf16[512]{0:T(512)(128)(2,1)S(1)}, bf16[512]{0:T(512)(128)(2,1)}, u32[]{:S(2)}) copy-start(bf16[512]{0:T(512)(128)(2,1)} %param.12) | copy-start | bytes 3076
  72.7 7.5 %copy-start.1 = (bf16[512]{0:T(512)(128)(2,1)S(1)}, bf16[512]{0:T(512)(128)(2,1)}, u32[]{:S(2)}) copy-start(bf16[512]{0:T(512)(128)(2,1)} %param.13) | copy-start | bytes 3076
  72.7 7.5 %copy-start.6 = (u32[256]{0:T(256)S(1)}, u32[256]{0:T(256)}, u32[]{:S(2)}) copy-start(u32[256]{0:T(256)} %constant.69) | copy-start | bytes 3076
  72.7 8.8 %copy-start.3 = (s32[4,2]{0,1:T(2,128)S(1)}, s32[4,2]{0,1:T(2,128)}, u32[]{:S(2)}) copy-start(s32[4,2]{0,1:T(2,128)} %param.15) | copy-start | bytes 100
  72.7 8.8 %copy-start.4 = (s32[4]{0:T(128)S(1)}, s32[4]{0:T(128)}, u32[]{:S(2)}) copy-start(s32[4]{0:T(128)} %param.16) | copy-start | bytes 52
  72.7 8.8 %copy-start.5 = (s32[4]{0:T(128)S(1)}, s32[4]{0:T(128)}, u32[]{:S(2)}) copy-start(s32[4]{0:T(128)} %param.14) | copy-start | bytes 52
  72.7 21.6 %all-to-all-start = ((bf16[16,16,512]{2,1,0:T(8,128)(2,1)}), bf16[16,16,512]{2,1,0:T(8,128)(2,1)}, u32[]{:S(2)}, u32[]{:S(2)}) async-start(bf16[16,16,512]{2,1,0:T(8,128)(2,1)} %bitcast.4), calls=%async_computation | async-start | bytes 524288 | tf_op jit(solution)/shard_map/all_to_all | solution.py:31
  94.3 28.9 %all-to-all-start.1 = ((bf16[16,16,512]{2,1,0:T(8,128)(2,1)}), bf16[16,16,512]{2,1,0:T(8,128)(2,1)S(1)}, u32[]{:S(2)}, u32[]{:S(2)}) async-start(bf16[16,16,512]{2,1,0:T(8,128)(2,1)} %all-to-all-done), calls=%async_computation.1 | async-start | bytes 524288 | tf_op jit(solution)/shard_map/all_to_all | solution.py:32
  99.2 175.6 %all-gather.8.cloned.1.call-start = ((), (), s32[]{:S(2)}) async-start(), calls=%async_computation.5 | async-start | bytes 4456448 | tf_op jit(solution)/shard_map/all_gather | solution.py:65
  274.7 3.4 %copy-start = (bf16[4096,512]{1,0:T(8,128)(2,1)S(1)}, bf16[4096,512]{1,0:T(8,128)(2,1)}, u32[]{:S(2)}) copy-start(bf16[4096,512]{1,0:T(8,128)(2,1)} %all-gather.6.cloned.1.call-done) | copy-start | bytes 12582916
Sparse Core Ops, SparseCore 0:
  9.8 44.7 all-gather.5
  72.8 81.7 reduce-scatter.1
  216.4 58.3 all-gather.7

commit v2 on v1

v2 whole, which is shorter than its diff:
```python
import jax
import jax.numpy as jnp
from jax import lax
from jax.experimental import pallas as pl
from jax.experimental.pallas import tpu as pltpu
from jax.sharding import Mesh
from jax.sharding import PartitionSpec as P

F32 = jnp.float32
BF16 = jnp.bfloat16
MESH = pl.DeviceIdType.MESH
WIDTH = 8192
HIGH = lax.Precision.HIGHEST


def wrap(value, size):
    return lax.rem(value + size, size)


def body(scale, attn_hbm, w_hbm, resid_hbm, vec, small, loss_ref, out_ref, gg_ref, gh_ref,
         att, wbuf, resbuf, res, vecr, smr, pf, m1s, m2s, m3s, m1r, m2r, m3r, s1f,
         n1s, n2s, n3s, n1r, n2r, n3r, zf, zt, za, hgc, stat, sa, sb, ks, cs, kc, gmine, gr, dt,
         loc_sem, att_txz, att_txc, att_rx, att_half, res_tx, res_rx, vec_sem, sm_tx, sm_rx,
         rs_tx, rs_rx, ag_tx, ag_rx, sa_tx, sa_rx, sb_tx, sb_rx, g_tx, g_rx):
    zc, core, x, y = (lax.axis_index(n) for n in ("z", "c", "x", "y"))
    r = zc * 2 + core
    t = x * 4 + y
    other = 1 - core
    zp, zm = wrap(zc + 1, 8), wrap(zc - 1, 8)
    diag = r == t

    def rep_dev(rr, tt):
        return {"z": rr // 2, "c": lax.rem(rr, 2), "x": tt // 4, "y": lax.rem(tt, 4)}

    def send(src, dst, tx, rx, dev):
        pltpu.make_async_remote_copy(src_ref=src, dst_ref=dst, send_sem=tx, recv_sem=rx,
                                     device_id=dev, device_id_type=MESH).start()

    def await_(ref, sem):
        pltpu.make_async_copy(ref, ref, sem).wait()

    load_a = pltpu.make_async_copy(attn_hbm, att.at[0, core], loc_sem.at[0])
    load_w = pltpu.make_async_copy(w_hbm.at[pl.ds(pl.multiple_of(r * 512, 512), 512)], wbuf, loc_sem.at[1])
    load_r = pltpu.make_async_copy(resid_hbm, resbuf, loc_sem.at[2])
    load_a.start()
    load_r.start()
    load_w.start()

    barrier = pltpu.get_barrier_semaphore()

    def greet(j, carry):
        pl.semaphore_signal(barrier, 1, device_id=rep_dev(wrap(r + j, 16), t), device_id_type=MESH)
        pl.semaphore_signal(barrier, 1, device_id=rep_dev(r, wrap(t + j, 16)), device_id_type=MESH)
        return carry

    lax.fori_loop(1, 16, greet, 0)

    def greet2(j, carry):
        @pl.when(jnp.logical_not(diag & (j == t)))
        def _():
            pl.semaphore_signal(barrier, 1, device_id=rep_dev(t, j), device_id_type=MESH)

        @pl.when(jnp.logical_not(diag & (j == r)))
        def _():
            pl.semaphore_signal(barrier, 1, device_id=rep_dev(j, r), device_id_type=MESH)

        return carry

    lax.fori_loop(0, 16, greet2, 0)
    pl.semaphore_wait(barrier, jnp.where(diag, 60, 62))

    load_a.wait()
    send(att.at[0, core], att.at[2, core], att_txz, att_rx.at[2, core], {"z": zp})
    send(att.at[0, core], att.at[1, core], att_txz, att_rx.at[1, core], {"z": zm})
    send(att.at[0, core], att.at[0, core], att_txc, att_rx.at[0, core], {"c": other})

    smr[r] = small[...]

    def send_small(j, carry):
        send(smr.at[r], smr.at[r], sm_tx, sm_rx, rep_dev(wrap(r + j, 16), t))
        return carry

    lax.fori_loop(1, 16, send_small, 0)

    @pl.when(diag)
    def _():
        vecr[...] = vec[...]

    @pl.when(jnp.logical_not(diag))
    def _():
        send(vec, vecr, vec_sem.at[0], vec_sem.at[1], rep_dev(t, r))

    load_r.wait()

    def send_res(j, carry):
        rows = pl.ds(pl.multiple_of(j * 16, 16), 16)
        own = diag & (j == t)

        @pl.when(own)
        def _():
            res[r] = resbuf[rows, :]

        @pl.when(jnp.logical_not(own))
        def _():
            send(resbuf.at[rows, :], res.at[r], res_tx, res_rx, rep_dev(t, j))

        return carry

    lax.fori_loop(0, 16, send_res, 0)
    load_w.wait()

    @pl.when(jnp.logical_not(diag))
    def _():
        await_(vecr, vec_sem.at[1])

    for q in range(4):
        row = vecr[q : q + 1, :] * vecr[4 + q : 5 + q, :]
        hgc[q] = jnp.broadcast_to(row, (128, 128)).T

    quarters = []
    for q in range(4):
        first = "x" if q < 2 else "y"
        second = "y" if q < 2 else "x"
        a0, b0 = (x, y) if q < 2 else (y, x)
        s = 1 if q % 2 == 0 else -1
        quarters.append(dict(
            q=q, a0=a0, b0=b0, lanes=slice(q * 128, (q + 1) * 128),
            af=wrap(a0 + 2, 4), an=wrap(a0 + s, 4), ao=wrap(a0 - s, 4),
            bf=wrap(b0 + 2, 4), bn=wrap(b0 + s, 4), bo=wrap(b0 - s, 4),
            dan={first: wrap(a0 + s, 4)}, dao={first: wrap(a0 - s, 4)},
            dbn={second: wrap(b0 + s, 4)}, dbo={second: wrap(b0 - s, 4)},
        ))

    def chunk(k, g, a):
        if g["q"] < 2:
            v = pf[k, :, pl.ds(a, 1), :, :, g["lanes"]]
        else:
            v = pf[k, :, :, pl.ds(a, 1), :, g["lanes"]]
        return v.reshape(2, 4, 16, 128)

    def tcol(g, a, b):
        return a * 4 + b if g["q"] < 2 else b * 4 + a

    def step_a(k):
        @pl.when((k == 1) | (k == 3))
        def _():
            await_(att.at[k, core], att_rx.at[k, core])
            send(att.at[k, core], att.at[k + 2, core], att_txz, att_rx.at[k + 2, core], {"z": zm})
            send(att.at[k, core], att.at[k, core], att_txc, att_rx.at[k, core], {"c": other})
            await_(att.at[k + 1, core], att_rx.at[k + 1, core])
            send(att.at[k + 1, core], att.at[k + 3, core], att_txz, att_rx.at[k + 3, core], {"z": zp})
            send(att.at[k + 1, core], att.at[k + 1, core], att_txc, att_rx.at[k + 1, core], {"c": other})

        @pl.when(k == 5)
        def _():
            lo, hi = pl.ds(0, 128), pl.ds(128, 128)
            await_(att.at[5, core], att_rx.at[5, core])
            send(att.at[5, core, hi], att.at[7, core, hi], att_txz, att_half, {"z": zm})
            send(att.at[5, core], att.at[5, core], att_txc, att_rx.at[5, core], {"c": other})
            await_(att.at[6, core], att_rx.at[6, core])
            send(att.at[6, core, lo], att.at[7, core, lo], att_txz, att_rx.at[7, core], {"z": zp})
            send(att.at[6, core], att.at[6, core], att_txc, att_rx.at[6, core], {"c": other})

        @pl.when(k == 7)
        def _():
            lo, hi = pl.ds(0, 128), pl.ds(128, 128)
            await_(att.at[7, core, lo], att_rx.at[7, core])
            await_(att.at[7, core, hi], att_half)
            send(att.at[7, core], att.at[7, core], att_txc, att_rx.at[7, core], {"c": other})

        await_(att.at[k, other], att_rx.at[k, other])
        rows = att[k].reshape(512, 512)
        prod = lax.dot_general(rows, wbuf[...], (((1,), (1,)), ((), ())), preferred_element_type=F32)
        pf[k] = prod.reshape(2, 4, 4, 16, 512)
        for g in quarters:
            q = g["q"]
            m1s[q, k] = chunk(k, g, g["af"]).astype(BF16)
            send(m1s.at[q, k], m1r.at[q, k], rs_tx.at[0, q], rs_rx.at[0, q, k], g["dan"])
        for g in quarters:
            q = g["q"]
            m3s[q, k] = chunk(k, g, g["ao"]).astype(BF16)
            send(m3s.at[q, k], m3r.at[q, k], rs_tx.at[1, q], rs_rx.at[1, q, k], g["dao"])

    def step_b(k):
        for g in quarters:
            q = g["q"]
            await_(m1r.at[q, k], rs_rx.at[0, q, k])
            m2s[q, k] = (chunk(k, g, g["an"]) + m1r[q, k].astype(F32)).astype(BF16)
            send(m2s.at[q, k], m2r.at[q, k], rs_tx.at[2, q], rs_rx.at[2, q, k], g["dan"])

    def step_c(k):
        for g in quarters:
            q = g["q"]
            await_(m3r.at[q, k], rs_rx.at[1, q, k])
            await_(m2r.at[q, k], rs_rx.at[2, q, k])
            s1f[q, k] = chunk(k, g, g["a0"]) + m2r[q, k].astype(F32) + m3r[q, k].astype(F32)
            n1s[q, k] = s1f[q, k, :, pl.ds(g["bf"], 1)].reshape(2, 16, 128).astype(BF16)
            send(n1s.at[q, k], n1r.at[q, k], rs_tx.at[3, q], rs_rx.at[3, q, k], g["dbn"])
            n3s[q, k] = s1f[q, k, :, pl.ds(g["bo"], 1)].reshape(2, 16, 128).astype(BF16)
            send(n3s.at[q, k], n3r.at[q, k], rs_tx.at[4, q], rs_rx.at[4, q, k], g["dbo"])

    def step_d(k):
        for g in quarters:
            q = g["q"]
            await_(n1r.at[q, k], rs_rx.at[3, q, k])
            n2s[q, k] = (s1f[q, k, :, pl.ds(g["bn"], 1)].reshape(2, 16, 128) + n1r[q, k].astype(F32)).astype(BF16)
            send(n2s.at[q, k], n2r.at[q, k], rs_tx.at[5, q], rs_rx.at[5, q, k], g["dbn"])

    def step_e(k):
        @pl.when(k == 0)
        def _():
            @pl.when(diag)
            def _():
                await_(res.at[pl.ds(0, 15)], res_rx)

            @pl.when(jnp.logical_not(diag))
            def _():
                await_(res, res_rx)

        off = ((k + 1) // 2) * (2 * lax.rem(k, 2) - 1)
        base = wrap(zc + off, 8) * 2
        for g in quarters:
            q = g["q"]
            await_(n2r.at[q, k], rs_rx.at[5, q, k])
            await_(n3r.at[q, k], rs_rx.at[4, q, k])
            total = s1f[q, k, :, pl.ds(g["b0"], 1)].reshape(2, 16, 128) + n2r[q, k].astype(F32) + n3r[q, k].astype(F32)
            zf[pl.ds(2 * k, 2), :, g["lanes"]] = total + res[pl.ds(base, 2), :, g["lanes"]].astype(F32)

    def flip(h):
        v = zf[8 * h : 8 * h + 8].reshape(128, 512)
        sq = jnp.zeros((1, 128), F32)
        dot = jnp.zeros((1, 128), F32)
        for q in range(4):
            turned = v[:, q * 128 : (q + 1) * 128].T
            zt[q, h] = turned
            za[h, t, q] = turned.astype(BF16)
            sq = sq + jnp.sum(turned * turned, axis=0, keepdims=True)
            dot = dot + jnp.sum(turned * hgc[q], axis=0, keepdims=True)
        stat[0:1, h * 128 : (h + 1) * 128] = sq
        stat[1:2, h * 128 : (h + 1) * 128] = dot

    def gsend(h, g, a, b, dev):
        q = g["q"]
        tt = tcol(g, a, b)
        send(za.at[h, tt, q], za.at[h, tt, q], ag_tx.at[q], ag_rx.at[h, q, tt], dev)

    def gwait(h, g, a, b):
        q = g["q"]
        tt = tcol(g, a, b)
        await_(za.at[h, tt, q], ag_rx.at[h, q, tt])

    def ag1(h):
        for g in quarters:
            gsend(h, g, g["a0"], g["b0"], g["dan"])
            gsend(h, g, g["a0"], g["b0"], g["dao"])
        for g in quarters:
            gsend(h, g, g["a0"], g["b0"], g["dbn"])
            gsend(h, g, g["a0"], g["b0"], g["dbo"])

    def ag2(h):
        for g in quarters:
            gwait(h, g, g["ao"], g["b0"])
            gsend(h, g, g["ao"], g["b0"], g["dan"])
        for g in quarters:
            gsend(h, g, g["ao"], g["b0"], g["dbn"])
            gsend(h, g, g["ao"], g["b0"], g["dbo"])
            gwait(h, g, g["an"], g["b0"])
            gsend(h, g, g["an"], g["b0"], g["dbn"])
            gsend(h, g, g["an"], g["b0"], g["dbo"])

    def ag3(h):
        for g in quarters:
            gwait(h, g, g["a0"], g["bo"])
            gsend(h, g, g["a0"], g["bo"], g["dbn"])
            gwait(h, g, g["af"], g["b0"])
            gsend(h, g, g["af"], g["b0"], g["dbn"])
            gsend(h, g, g["af"], g["b0"], g["dbo"])

    def ag4(h):
        for g in quarters:
            for a in ("ao", "an", "af"):
                gwait(h, g, g[a], g["bo"])
                gsend(h, g, g[a], g["bo"], g["dbn"])

    def ag5(h):
        for g in quarters:
            for a in ("a0", "ao", "an", "af"):
                gwait(h, g, g[a], g["bn"])
                gwait(h, g, g[a], g["bf"])

    def step(i, carry):
        @pl.when(i >= 4)
        def _():
            step_e(i - 4)

        @pl.when((i >= 3) & (i < 11))
        def _():
            step_d(i - 3)

        @pl.when((i >= 2) & (i < 10))
        def _():
            step_c(i - 2)

        @pl.when((i >= 1) & (i < 9))
        def _():
            step_b(i - 1)

        @pl.when(i < 8)
        def _():
            step_a(i)

        @pl.when(i == 7)
        def _():
            flip(0)
            ag1(0)

        @pl.when(i == 9)
        def _():
            ag2(0)

        @pl.when(i == 10)
        def _():
            ag3(0)

        @pl.when(i == 11)
        def _():
            ag4(0)

        return carry

    stat[...] = jnp.zeros((8, 256), F32)
    lax.fori_loop(0, 12, step, 0)
    flip(1)

    def absolute(lane):
        slot = lane >> 4
        k = slot >> 1
        off = ((k + 1) >> 1) * (2 * (k & 1) - 1)
        return ((((zc + off + 8) & 7) * 2 + (slot & 1)) << 4) + (lane & 15)

    rows256 = lax.broadcasted_iota(jnp.int32, (256, 256), 0)
    cols256 = lax.broadcasted_iota(jnp.int32, (256, 256), 1)
    to_abs = (absolute(rows256) == cols256).astype(F32)
    moved = jnp.dot(stat[...], to_abs, precision=HIGH, preferred_element_type=F32)
    sa[r] = jnp.zeros((8, 128), F32)
    sa[r, 0:1, :] = moved[0:1, 0:128]
    sa[r, 1:2, :] = moved[0:1, 128:256]
    sa[r, 2:3, :] = moved[1:2, 0:128]
    sa[r, 3:4, :] = moved[1:2, 128:256]

    def send_sa(j, carry):
        send(sa.at[r], sa.at[r], sa_tx, sa_rx, rep_dev(wrap(r + j, 16), t))
        return carry

    lax.fori_loop(1, 16, send_sa, 0)
    ag1(1)
    ag2(1)
    await_(sa.at[pl.ds(0, 15)], sa_rx)
    sb[t] = jnp.sum(sa[...], axis=0)

    def send_sb(j, carry):
        send(sb.at[t], sb.at[t], sb_tx, sb_rx, rep_dev(r, wrap(t + j, 16)))
        return carry

    lax.fori_loop(1, 16, send_sb, 0)
    ag3(1)
    await_(smr.at[pl.ds(0, 15)], sm_rx)
    await_(sb.at[pl.ds(0, 15)], sb_rx)

    ints = smr[:, 0, :].astype(F32)
    tsub = lax.broadcasted_iota(jnp.int32, (16, 128), 0)
    lane = lax.broadcasted_iota(jnp.int32, (16, 128), 1)
    group_r = lax.broadcasted_iota(jnp.int32, (16, 128), 0)
    bl_r = lax.broadcasted_iota(jnp.int32, (128, 128), 0)
    bl_c = lax.broadcasted_iota(jnp.int32, (128, 128), 1)
    block = ((bl_r >> 4) == (bl_c >> 4)).astype(F32)
    eight = lax.broadcasted_iota(jnp.int32, (8, 128), 0)
    halves = []
    count = jnp.zeros((1, 1), F32)
    loss_sum = jnp.zeros((1, 1), F32)
    for h in range(2):
        spread = ((lane >> 4) + 8 * h == group_r).astype(F32)
        ex = lax.dot_general(ints, spread, (((0,), (0,)), ((), ())), precision=HIGH, preferred_element_type=F32)
        lens = [ex[i : i + 1, :] for i in range(4)]
        firsts = [ex[4 + i : 5 + i, :] for i in range(4)]
        seconds = [ex[8 + i : 9 + i, :] for i in range(4)]
        valid = [ex[12 + i : 13 + i, :] for i in range(4)]
        inv = 1.0 / jnp.sqrt(sb[:, h, :] / WIDTH + 1e-05)
        score = inv * sb[:, 2 + h, :]
        lens16 = jnp.zeros((16, 128), F32)
        for i in range(4):
            lens16 = lens16 + jnp.where((tsub >> 2) == i, lens[i], 0.0)
        within = ((tsub & 3) * 16 + (lane & 15)).astype(F32)
        live = (within < lens16).astype(F32)
        pooled = score * live
        stack = jnp.zeros((8, 128), F32)
        for i in range(4):
            part = jnp.sum(jnp.where((tsub >> 2) == i, pooled, 0.0), axis=0, keepdims=True)
            stack = stack + jnp.where(eight == i, part, 0.0)
        summed = jnp.dot(stack, block, precision=HIGH, preferred_element_type=F32)
        reward = [summed[i : i + 1, :] / lens[i] for i in range(4)]
        weights = []
        for p in range(4):
            margin = jnp.zeros((1, 128), F32)
            for i in range(4):
                margin = margin + jnp.where(firsts[p] == i, reward[i], 0.0) - jnp.where(seconds[p] == i, reward[i], 0.0)
            soft = jnp.maximum(-margin, 0.0) + jnp.log1p(jnp.exp(-jnp.abs(margin)))
            loss_sum = loss_sum + jnp.sum(valid[p] * soft, axis=1, keepdims=True) * (1.0 / 16.0)
            count = count + jnp.sum(valid[p], axis=1, keepdims=True) * (1.0 / 16.0)
            weights.append(valid[p] / (1.0 + jnp.exp(margin)))
        halves.append((lens, firsts, seconds, inv, score, live, weights))
    loss_ref[...] = jnp.broadcast_to(loss_sum / count, (8, 128))
    factor = -scale[0] / count
    for h in range(2):
        lens, firsts, seconds, inv, score, live, weights = halves[h]
        dscore = jnp.zeros((16, 128), F32)
        for i in range(4):
            d = jnp.zeros((1, 128), F32)
            for p in range(4):
                w = weights[p] * factor
                d = d + jnp.where(firsts[p] == i, w, 0.0) - jnp.where(seconds[p] == i, w, 0.0)
            dscore = dscore + jnp.where((tsub >> 2) == i, d / lens[i], 0.0)
        dscore = dscore * live
        ks[:, h * 128 : (h + 1) * 128] = inv * dscore
        cs[:, h * 128 : (h + 1) * 128] = inv * inv * dscore * score * (1.0 / WIDTH)
    to_slot = (rows256 == absolute(cols256)).astype(F32)
    kslot = jnp.dot(ks[...], to_slot, precision=HIGH, preferred_element_type=F32)
    cslot = jnp.dot(cs[...], to_slot, precision=HIGH, preferred_element_type=F32)
    for i in range(16):
        kc[i, 0:1, :] = kslot[i : i + 1, :]
        kc[i, 1:2, :] = cslot[i : i + 1, :]

    krow = [kc[t, 0:1, 0:128], kc[t, 0:1, 128:256]]
    gsum = jnp.zeros((8, 128), F32)
    for q in range(4):
        prod = zt[q, 0] * krow[0] + zt[q, 1] * krow[1]
        row = jnp.sum(prod.T, axis=0, keepdims=True)
        gsum = gsum + jnp.where(eight == q, row, 0.0)
    gmine[...] = gsum

    def send_g(j, carry):
        own = diag & (j == r)

        @pl.when(own)
        def _():
            gr[t] = gmine[...]

        @pl.when(jnp.logical_not(own))
        def _():
            send(gmine, gr.at[t], g_tx, g_rx, rep_dev(j, r))

        return carry

    lax.fori_loop(0, 16, send_g, 0)
    ag4(1)

    def contract(h, first):
        def group(gi, carry):
            parts = []
            for j in range(4):
                tt = gi * 4 + j
                k1 = kc[tt, 0:1, h * 128 : (h + 1) * 128]
                c1 = kc[tt, 1:2, h * 128 : (h + 1) * 128]
                for q in range(4):
                    val = hgc[q] * k1 - za[h, tt, q].astype(F32) * c1
                    dt[q * 128 : (q + 1) * 128, j * 128 : (j + 1) * 128] = val.astype(BF16)
                parts.append(att[4 * h : 4 * h + 4, :, pl.ds(pl.multiple_of(tt * 16, 16), 16), :].reshape(128, 512))
            rhs = jnp.concatenate(parts, axis=0)
            prod = jnp.dot(dt[...], rhs, preferred_element_type=F32)

            if first:
                @pl.when(gi == 0)
                def _():
                    out_ref[...] = prod

                @pl.when(gi > 0)
                def _():
                    out_ref[...] += prod
            else:
                out_ref[...] += prod
            return carry

        lax.fori_loop(0, 4, group, 0)

    ag5(0)
    contract(0, True)
    ag5(1)
    contract(1, False)

    @pl.when(diag)
    def _():
        await_(gr.at[pl.ds(0, 15)], g_rx)
        await_(gr.at[pl.ds(0, 15)], g_tx)
        await_(res.at[pl.ds(0, 15)], res_tx)

    @pl.when(jnp.logical_not(diag))
    def _():
        await_(gr, g_rx)
        await_(gr, g_tx)
        await_(res, res_tx)
        await_(vecr, vec_sem.at[0])

    total = jnp.sum(gr[...], axis=0)
    gg_ref[...] = total[0:4, :] * vec[4:8, :]
    gh_ref[...] = total[0:4, :] * vec[0:4, :]

    await_(att.at[pl.ds(0, 7), 0], att_txz)
    await_(att.at[:, 0], att_txc)
    await_(smr.at[pl.ds(0, 15)], sm_tx)
    await_(sa.at[pl.ds(0, 15)], sa_tx)
    await_(sb.at[pl.ds(0, 15)], sb_tx)
    for q in range(4):
        for i, buf in enumerate((m1s, m3s, m2s, n1s, n3s, n2s)):
            await_(buf.at[q], rs_tx.at[i, q])
        await_(za.at[:, pl.ds(0, 15), q], ag_tx.at[q])


def shards(attn, out_weight, resid, norm_gain, head, lengths, pairs, pair_valid, loss_scale):
    vec = jnp.concatenate([norm_gain, head]).astype(F32).reshape(8, 128)
    small = jnp.concatenate([lengths, pairs[:, 0], pairs[:, 1], pair_valid])
    small = jnp.pad(small, (0, 1024 - small.shape[0])).reshape(8, 128)
    vm = pltpu.VMEM
    dma = pltpu.SemaphoreType.DMA
    big = (4, 8, 2, 4, 16, 128)
    little = (4, 8, 2, 16, 128)
    vspec = pl.BlockSpec(memory_space=pltpu.VMEM)
    anyspec = pl.BlockSpec(memory_space=pl.ANY)
    loss, out, gg, gh = pl.pallas_call(
        body,
        name="whole",
        out_shape=(
            jax.ShapeDtypeStruct((8, 128), F32),
            jax.ShapeDtypeStruct((512, 512), F32),
            jax.ShapeDtypeStruct((4, 128), F32),
            jax.ShapeDtypeStruct((4, 128), F32),
        ),
        in_specs=[pl.BlockSpec(memory_space=pltpu.SMEM), anyspec, anyspec, anyspec, vspec, vspec],
        out_specs=(vspec, vspec, vspec, vspec),
        scratch_shapes=[
            vm((8, 2, 256, 512), BF16), vm((512, 512), BF16), vm((256, 512), BF16), vm((16, 16, 512), BF16),
            vm((8, 128), F32), vm((16, 8, 128), jnp.int32), vm((8, 2, 4, 4, 16, 512), F32),
            vm(big, BF16), vm(big, BF16), vm(big, BF16), vm(big, BF16), vm(big, BF16), vm(big, BF16), vm(big, F32),
            vm(little, BF16), vm(little, BF16), vm(little, BF16), vm(little, BF16), vm(little, BF16), vm(little, BF16),
            vm((16, 16, 512), F32), vm((4, 2, 128, 128), F32), vm((2, 16, 4, 128, 128), BF16), vm((4, 128, 128), F32),
            vm((8, 256), F32), vm((16, 8, 128), F32), vm((16, 8, 128), F32), vm((16, 256), F32), vm((16, 256), F32), vm((16, 8, 256), F32),
            vm((8, 128), F32), vm((16, 8, 128), F32), vm((512, 512), BF16),
            dma((3,)), dma, dma, dma((8, 2)), dma, dma, dma, dma((2,)), dma, dma,
            dma((6, 4)), dma((6, 4, 8)), dma((4,)), dma((2, 4, 16)), dma, dma, dma, dma, dma, dma,
        ],
        compiler_params=pltpu.CompilerParams(collective_id=0, has_side_effects=True, vmem_limit_bytes=60 * 1024 * 1024),
    )(loss_scale, attn, out_weight, resid, vec, small)
    return (loss[0, 0:1], out, gg.reshape(512), gh.reshape(512))


def solution(mesh):
    finer = Mesh(mesh.devices.reshape(8, 2, 4, 4), ("z", "c", "x", "y"))
    rep, ten = ("z", "c"), ("x", "y")
    placed = (P(rep, ten), P(None, ten), P(rep, ten), P(ten), P(ten), P(rep), P(rep, None), P(rep), P())
    return jax.shard_map(
        shards,
        mesh=finer,
        in_specs=placed,
        out_specs=(P(), P(rep, ten), P(ten), P(ten)),
        check_vma=False,
    )
```

time: 291 us -> 127 us (0.44)
  blocking collectives: 138 us -> 0 us
  Pallas kernels: 0 us -> 115 us
  waiting for transfers between devices: 89.7 us -> 0 us
  between operations: 17.8 us -> 1.29 us
  starting transfers between devices: 12.4 us -> 0 us
  matrix products: 10 us -> 0 us
  local copies, waits for them, and re-layouts: 16 us -> 7.32 us
  other arithmetic: 5.51 us -> 2.04 us
    pallas_call x0 -> x1, Pallas kernels: none -> 115 us  [shards(): pl.pallas_call(body, name='whole', out_shape=(jax.ShapeDtypeStruct((8, 12...]
    psum x3 -> x0, blocking collectives: 88.1 us -> none  [the longest x1 32.8 us: shards(): lax.psum(pool[:, None] * onehot[None, :], 'tensor') / lens_all.astype(f32)]
    all_gather x2 -> x0, waiting for transfers between devices: 57.6 us -> none  [the longest x1 46.7 us: shards(): attn_all = lax.all_gather(attn, REP, axis=0, tiled=True)]
    all_gather x2 -> x0, blocking collectives: 37.2 us -> none  [the longest x1 23 us: shards(): vec_all = lax.all_gather(vec, 'tensor', axis=1, tiled=True)]
    reduce_scatter x1 -> x0, waiting for transfers between devices: 31.4 us -> none  [shards(): proj = lax.psum_scatter(part_sum, 'tensor', scatter_dimension=0, tiled=True)]
    unnamed x1 -> x0, blocking collectives: 12.5 us -> none
    all_to_all x2 -> x0, starting transfers between devices: 12.2 us -> none  [the longest x1 7.42 us: shards(): lax.all_to_all(resid, 'tensor', split_axis=0, concat_axis=0, tiled=True)]
    dot_general x2 -> x0, matrix products: 10 us -> none  [the longest x1 6.7 us: shards(): lax.dot_general(attn_all, w, (((1,), (1,)), ((), ())), preferred_element_...]
  transfers between devices with their start and end apart: 5 -> 0, of which waited for: 3 -> 0; matrix products, arithmetic and copies ran while one was open for 1% -> 0% of each run, Pallas kernels for 0% -> 0%
where the time goes in v2:
time: 127 us; the launch traced here: 126 us
  Pallas kernels  115 us (91%)
  local copies, waits for them, and re-layouts  7.32 us (6%)
  other arithmetic  2.04 us (2%)
  between operations  1.29 us (1%)
    pallas_call x1, Pallas kernels, shards(): pl.pallas_call(body, name='whole', out_shape=(jax.ShapeDtypeStruct((8, 12...  115 us
    unnamed x3, local copies, waits for them, and re-layouts  4.78 us

profile of v2, /device:TPU:4, one launch (start us, length us, event | category | flops | bytes accessed | tf_op | source)
XLA Modules:
  0.0 125.7 jit_solution(14275252810778985244)
XLA Ops:
  1.3 0.8 slice_bitcast_fusion.1
  2.0 0.7 pad_add_fusion
  2.8 0.6 pad_bitcast_fusion.small
  3.4 1.3 %maximum_convert_fusion.vec = f32[8,128]{1,0:T(8,128)} fusion(bf16[4,128]{1,0:T(4,128)(2,1)} %bitcast.13, bf16[4,128]{1,0:T(4,128)(2,1)} %bitcast.14), kind=kLoop, calls=%fused_computation.1 | loop fusion | flops 4096 | bytes 6144 | tf_op jit(solution)/shard_map/convert_element_type | solution.py:519
  4.7 115.0 %whole.1 = (f32[8,128]{1,0:T(8,128)}, f32[512,512]{1,0:T(8,128)}, f32[4,128]{1,0:T(4,128)}, f32[4,128]{1,0:T(4,128)}) custom-call(f32[1]{0:T(128)S(6)} %copy.16.scale, bf16[256,512]{1,0:T(8,128)(2,1)} %attn_hbm.1, bf16[8192,512]{1,0:T(8,128)(2,1)} %w_hbm.1, bf16[256,512]{1,0:T(8,128)(2,1)} %resid_hbm.1, f32[8,128]{1,0:T(8,128)} %maximum_convert_fusion.vec, ...), custom_call_target="tpu_custom_call" | custom-call | tf_op jit(solution)/shard_map/whole/pallas_call | solution.py:528
  119.7 1.2 slice.11
  120.9 2.3 %copy.17 = f32[512,512]{1,0:T(8,128)} copy(f32[512,512]{1,0:T(8,128)} %get-tuple-element.19) | data formatting | bytes 2097152
  123.2 1.3 copy.18
  124.4 1.3 %copy.19 = f32[512]{0:T(512)} copy(f32[512]{0:T(512)} %bitcast.11) | data formatting | bytes 4096

commit v3 on v2

--- a/solution.py
+++ b/solution.py
@@ -17,10 +17,10 @@
     return lax.rem(value + size, size)
 
 
-def body(scale, attn_hbm, w_hbm, resid_hbm, vec, small, loss_ref, out_ref, gg_ref, gh_ref,
-         att, wbuf, resbuf, res, vecr, smr, pf, m1s, m2s, m3s, m1r, m2r, m3r, s1f,
-         n1s, n2s, n3s, n1r, n2r, n3r, zf, zt, za, hgc, stat, sa, sb, ks, cs, kc, gmine, gr, dt,
-         loc_sem, att_txz, att_txc, att_rx, att_half, res_tx, res_rx, vec_sem, sm_tx, sm_rx,
+def body(scale, lens_ref, pairs_ref, valid_ref, attn_hbm, w_hbm, resid_hbm, gain_ref, head_ref, out_ref, misc_ref,
+         att, wbuf, resbuf, rx, zo, zin, vec, vall, hgr, acc, smr, pf, m1s, m2s, m3s, m1r, m2r, m3r, s1f,
+         n1s, n2s, n3s, n1r, n2r, n3r, zt, za, hgc, sa, sb, ks, cs, kc, gmine, gr, dt,
+         loc_sem, w_sem, att_txz, att_txc, att_rx, att_rxc, r1_tx, r1_rx, zin_tx, zin_rx, vec_tx, vec_rx, sm_tx, sm_rx,
          rs_tx, rs_rx, ag_tx, ag_rx, sa_tx, sa_rx, sb_tx, sb_rx, g_tx, g_rx):
     zc, core, x, y = (lax.axis_index(n) for n in ("z", "c", "x", "y"))
     r = zc * 2 + core
@@ -40,11 +40,22 @@
         pltpu.make_async_copy(ref, ref, sem).wait()
 
     load_a = pltpu.make_async_copy(attn_hbm, att.at[0, core], loc_sem.at[0])
-    load_w = pltpu.make_async_copy(w_hbm.at[pl.ds(pl.multiple_of(r * 512, 512), 512)], wbuf, loc_sem.at[1])
-    load_r = pltpu.make_async_copy(resid_hbm, resbuf, loc_sem.at[2])
+    load_r = pltpu.make_async_copy(resid_hbm, resbuf, loc_sem.at[1])
     load_a.start()
+
+    def offset(k):
+        return ((k + 1) // 2) * (2 * lax.rem(k, 2) - 1)
+
+    def aim(k):
+        return wrap(zc - offset(k), 8)
+
+    def load_w(k, carry):
+        rows = pl.ds(pl.multiple_of(aim(k) * 1024, 1024), 1024)
+        pltpu.make_async_copy(w_hbm.at[rows], wbuf.at[k], w_sem.at[k]).start()
+        return carry
+
+    lax.fori_loop(0, 8, load_w, 0)
     load_r.start()
-    load_w.start()
 
     barrier = pltpu.get_barrier_semaphore()
 
@@ -70,52 +81,55 @@
     pl.semaphore_wait(barrier, jnp.where(diag, 60, 62))
 
     load_a.wait()
-    send(att.at[0, core], att.at[2, core], att_txz, att_rx.at[2, core], {"z": zp})
-    send(att.at[0, core], att.at[1, core], att_txz, att_rx.at[1, core], {"z": zm})
-    send(att.at[0, core], att.at[0, core], att_txc, att_rx.at[0, core], {"c": other})
-
-    smr[r] = small[...]
-
-    def send_small(j, carry):
-        send(smr.at[r], smr.at[r], sm_tx, sm_rx, rep_dev(wrap(r + j, 16), t))
-        return carry
-
-    lax.fori_loop(1, 16, send_small, 0)
-
-    @pl.when(diag)
-    def _():
-        vecr[...] = vec[...]
-
-    @pl.when(jnp.logical_not(diag))
-    def _():
-        send(vec, vecr, vec_sem.at[0], vec_sem.at[1], rep_dev(t, r))
-
-    load_r.wait()
-
-    def send_res(j, carry):
-        rows = pl.ds(pl.multiple_of(j * 16, 16), 16)
-        own = diag & (j == t)
-
-        @pl.when(own)
-        def _():
-            res[r] = resbuf[rows, :]
-
-        @pl.when(jnp.logical_not(own))
-        def _():
-            send(resbuf.at[rows, :], res.at[r], res_tx, res_rx, rep_dev(t, j))
-
-        return carry
-
-    lax.fori_loop(0, 16, send_res, 0)
-    load_w.wait()
-
-    @pl.when(jnp.logical_not(diag))
-    def _():
-        await_(vecr, vec_sem.at[1])
-
-    for q in range(4):
-        row = vecr[q : q + 1, :] * vecr[4 + q : 5 + q, :]
-        hgc[q] = jnp.broadcast_to(row, (128, 128)).T
+    def rows_of(j):
+        return pl.ds(pl.multiple_of(j * 64, 64), 64)
+
+    def up(k, j):
+        return att.at[k, core, rows_of(lax.rem(j + 2, 4))]
+
+    def down(k, j):
+        return att.at[k, core, rows_of(j)]
+
+    def send_own(j, carry):
+        send(up(0, j), up(1, j), att_txz, att_rx.at[1, j], {"z": zm})
+        send(down(0, j), down(2, j), att_txz, att_rx.at[2, j], {"z": zp})
+        return carry
+
+    lax.fori_loop(0, 4, send_own, 0)
+    send(att.at[0, core], att.at[0, core], att_txc, att_rxc.at[0], {"c": other})
+
+    def spread():
+        lane8 = lax.broadcasted_iota(jnp.int32, (8, 128), 1)
+        ints8 = jnp.zeros((8, 128), jnp.int32)
+        for i in range(4):
+            ints8 = jnp.where(lane8 == i, lens_ref[i], ints8)
+            ints8 = jnp.where(lane8 == 4 + i, pairs_ref[0, i], ints8)
+            ints8 = jnp.where(lane8 == 8 + i, pairs_ref[1, i], ints8)
+            ints8 = jnp.where(lane8 == 12 + i, valid_ref[i], ints8)
+        smr[r] = ints8
+        vec[0:4, :] = gain_ref[...].astype(F32).reshape(4, 128)
+        vec[4:8, :] = head_ref[...].astype(F32).reshape(4, 128)
+        vall[t] = vec[...]
+        load_r.wait()
+        rx[t] = resbuf[pl.ds(pl.multiple_of(t * 16, 16), 16), :]
+        acc[...] = jnp.zeros((2, 16, 128), F32)
+
+        def one(j, carry):
+            tt = wrap(t + j, 16)
+            rows = pl.ds(pl.multiple_of(tt * 16, 16), 16)
+            send(smr.at[r], smr.at[r], sm_tx, sm_rx, rep_dev(wrap(r + j, 16), t))
+            send(vec, vall.at[t], vec_tx, vec_rx, rep_dev(r, tt))
+            send(resbuf.at[rows, :], rx.at[t], r1_tx, r1_rx, rep_dev(r, tt))
+            return carry
+
+        lax.fori_loop(1, 16, one, 0)
+
+    def gathered():
+        await_(vall.at[pl.ds(0, 15)], vec_rx)
+        await_(rx.at[pl.ds(0, 15)], r1_rx)
+        hgr[...] = vall[:, 0:4, :] * vall[:, 4:8, :]
+        for q in range(4):
+            hgc[q] = jnp.broadcast_to(hgr[r, q : q + 1, :], (128, 128)).T
 
     quarters = []
     for q in range(4):
@@ -141,37 +155,50 @@
     def tcol(g, a, b):
         return a * 4 + b if g["q"] < 2 else b * 4 + a
 
+    def ring(n):
+        d, j = n // 4 + 1, lax.rem(n, 4)
+        kp, km = 2 * d - 1, 2 * d
+
+        @pl.when(n < 8)
+        def _():
+            await_(up(kp, j), att_rx.at[kp, j])
+            send(up(kp, j), up(kp + 2, j), att_txz, att_rx.at[kp + 2, j], {"z": zm})
+            await_(down(km, j), att_rx.at[km, j])
+            send(down(km, j), down(km + 2, j), att_txz, att_rx.at[km + 2, j], {"z": zp})
+
+        @pl.when((n >= 8) & (n < 12))
+        def _():
+            await_(up(5, j), att_rx.at[5, j])
+
+            @pl.when(j < 2)
+            def _():
+                send(up(5, j), up(7, j), att_txz, att_rx.at[7, j], {"z": zm})
+
+            await_(down(6, j), att_rx.at[6, j])
+
+            @pl.when(j < 2)
+            def _():
+                send(down(6, j), down(7, j), att_txz, att_rx.at[7, j + 2], {"z": zp})
+
+        @pl.when((j == 3) & (n < 12))
+        def _():
+            send(att.at[kp, core], att.at[kp, core], att_txc, att_rxc.at[kp], {"c": other})
+            send(att.at[km, core], att.at[km, core], att_txc, att_rxc.at[km], {"c": other})
+
+        @pl.when(n >= 12)
+        def _():
+            await_(up(7, j), att_rx.at[7, j])
+            await_(down(7, j), att_rx.at[7, j + 2])
+
+            @pl.when(j == 1)
+            def _():
+                send(att.at[7, core], att.at[7, core], att_txc, att_rxc.at[7], {"c": other})
+
     def step_a(k):
-        @pl.when((k == 1) | (k == 3))
-        def _():
-            await_(att.at[k, core], att_rx.at[k, core])
-            send(att.at[k, core], att.at[k + 2, core], att_txz, att_rx.at[k + 2, core], {"z": zm})
-            send(att.at[k, core], att.at[k, core], att_txc, att_rx.at[k, core], {"c": other})
-            await_(att.at[k + 1, core], att_rx.at[k + 1, core])
-            send(att.at[k + 1, core], att.at[k + 3, core], att_txz, att_rx.at[k + 3, core], {"z": zp})
-            send(att.at[k + 1, core], att.at[k + 1, core], att_txc, att_rx.at[k + 1, core], {"c": other})
-
-        @pl.when(k == 5)
-        def _():
-            lo, hi = pl.ds(0, 128), pl.ds(128, 128)
-            await_(att.at[5, core], att_rx.at[5, core])
-            send(att.at[5, core, hi], att.at[7, core, hi], att_txz, att_half, {"z": zm})
-            send(att.at[5, core], att.at[5, core], att_txc, att_rx.at[5, core], {"c": other})
-            await_(att.at[6, core], att_rx.at[6, core])
-            send(att.at[6, core, lo], att.at[7, core, lo], att_txz, att_rx.at[7, core], {"z": zp})
-            send(att.at[6, core], att.at[6, core], att_txc, att_rx.at[6, core], {"c": other})
-
-        @pl.when(k == 7)
-        def _():
-            lo, hi = pl.ds(0, 128), pl.ds(128, 128)
-            await_(att.at[7, core, lo], att_rx.at[7, core])
-            await_(att.at[7, core, hi], att_half)
-            send(att.at[7, core], att.at[7, core], att_txc, att_rx.at[7, core], {"c": other})
-
-        await_(att.at[k, other], att_rx.at[k, other])
-        rows = att[k].reshape(512, 512)
-        prod = lax.dot_general(rows, wbuf[...], (((1,), (1,)), ((), ())), preferred_element_type=F32)
-        pf[k] = prod.reshape(2, 4, 4, 16, 512)
+        await_(wbuf.at[k], w_sem.at[k])
+        prod = lax.dot_general(att[0, core], wbuf[k], (((1,), (1,)), ((), ())), preferred_element_type=F32)
+        pf[k, 0] = prod[:, 0:512].reshape(4, 4, 16, 512)
+        pf[k, 1] = prod[:, 512:1024].reshape(4, 4, 16, 512)
         for g in quarters:
             q = g["q"]
             m1s[q, k] = chunk(k, g, g["af"]).astype(BF16)
@@ -207,37 +234,40 @@
             send(n2s.at[q, k], n2r.at[q, k], rs_tx.at[5, q], rs_rx.at[5, q, k], g["dbn"])
 
     def step_e(k):
-        @pl.when(k == 0)
-        def _():
-            @pl.when(diag)
-            def _():
-                await_(res.at[pl.ds(0, 15)], res_rx)
-
-            @pl.when(jnp.logical_not(diag))
-            def _():
-                await_(res, res_rx)
-
-        off = ((k + 1) // 2) * (2 * lax.rem(k, 2) - 1)
-        base = wrap(zc + off, 8) * 2
+        dz = aim(k)
+        sq = jnp.zeros((16, 128), F32)
+        dot = jnp.zeros((16, 128), F32)
         for g in quarters:
             q = g["q"]
             await_(n2r.at[q, k], rs_rx.at[5, q, k])
             await_(n3r.at[q, k], rs_rx.at[4, q, k])
             total = s1f[q, k, :, pl.ds(g["b0"], 1)].reshape(2, 16, 128) + n2r[q, k].astype(F32) + n3r[q, k].astype(F32)
-            zf[pl.ds(2 * k, 2), :, g["lanes"]] = total + res[pl.ds(base, 2), :, g["lanes"]].astype(F32)
+            total = total + rx[pl.ds(2 * dz, 2), :, g["lanes"]].astype(F32)
+            for cc in range(2):
+                sq = sq + total[cc] * total[cc]
+                dot = dot + total[cc] * hgr[2 * dz + cc, q : q + 1, :]
+            zo[k, :, :, g["lanes"]] = total.astype(BF16)
+        acc[0] += sq
+        acc[1] += dot
+        h = k // 4
+
+        @pl.when(k == 0)
+        def _():
+            zin[core] = zo[0, core]
+
+        @pl.when(k > 0)
+        def _():
+            send(zo.at[k, core], zin.at[2 * k + core], zin_tx.at[h], zin_rx.at[h], {"z": dz})
+
+        send(zo.at[k, other], zin.at[2 * k + core], zin_tx.at[h], zin_rx.at[h], {"z": dz, "c": other})
 
     def flip(h):
-        v = zf[8 * h : 8 * h + 8].reshape(128, 512)
-        sq = jnp.zeros((1, 128), F32)
-        dot = jnp.zeros((1, 128), F32)
+        await_(zin.at[pl.ds(0, 7 + h)], zin_rx.at[h])
+        v = zin[8 * h : 8 * h + 8].reshape(128, 512).astype(F32)
         for q in range(4):
             turned = v[:, q * 128 : (q + 1) * 128].T
             zt[q, h] = turned
             za[h, t, q] = turned.astype(BF16)
-            sq = sq + jnp.sum(turned * turned, axis=0, keepdims=True)
-            dot = dot + jnp.sum(turned * hgc[q], axis=0, keepdims=True)
-        stat[0:1, h * 128 : (h + 1) * 128] = sq
-        stat[1:2, h * 128 : (h + 1) * 128] = dot
 
     def gsend(h, g, a, b, dev):
         q = g["q"]
@@ -288,49 +318,48 @@
                 gwait(h, g, g[a], g["bn"])
                 gwait(h, g, g[a], g["bf"])
 
-    def step(i, carry):
-        @pl.when(i >= 4)
-        def _():
-            step_e(i - 4)
-
-        @pl.when((i >= 3) & (i < 11))
-        def _():
-            step_d(i - 3)
-
-        @pl.when((i >= 2) & (i < 10))
-        def _():
-            step_c(i - 2)
-
-        @pl.when((i >= 1) & (i < 9))
-        def _():
-            step_b(i - 1)
-
-        @pl.when(i < 8)
-        def _():
-            step_a(i)
-
-        @pl.when(i == 7)
+    def on(n, parity, first, fn):
+        k = (n - first) // 2
+
+        @pl.when((lax.rem(n, 2) == parity) & (n >= first) & (n < first + 16))
+        def _():
+            fn(k)
+
+    def step(n, carry):
+        @pl.when(n == 12)
+        def _():
+            gathered()
+
+        on(n, 0, 12, step_e)
+        on(n, 1, 9, step_d)
+        on(n, 0, 6, step_c)
+        on(n, 1, 3, step_b)
+        on(n, 0, 0, step_a)
+
+        @pl.when(n == 1)
+        def _():
+            spread()
+
+        @pl.when((n >= 7) & (n < 21))
+        def _():
+            ring(n - 7)
+
+        @pl.when(n == 21)
         def _():
             flip(0)
             ag1(0)
 
-        @pl.when(i == 9)
+        @pl.when(n == 24)
         def _():
             ag2(0)
 
-        @pl.when(i == 10)
+        @pl.when(n == 25)
         def _():
             ag3(0)
 
-        @pl.when(i == 11)
-        def _():
-            ag4(0)
-
-        return carry
-
-    stat[...] = jnp.zeros((8, 256), F32)
-    lax.fori_loop(0, 12, step, 0)
-    flip(1)
+        return carry
+
+    lax.fori_loop(0, 27, step, 0)
 
     def absolute(lane):
         slot = lane >> 4
@@ -340,29 +369,37 @@
 
     rows256 = lax.broadcasted_iota(jnp.int32, (256, 256), 0)
     cols256 = lax.broadcasted_iota(jnp.int32, (256, 256), 1)
-    to_abs = (absolute(rows256) == cols256).astype(F32)
-    moved = jnp.dot(stat[...], to_abs, precision=HIGH, preferred_element_type=F32)
+    lane16 = lax.broadcasted_iota(jnp.int32, (16, 128), 1)
+    row16 = lax.broadcasted_iota(jnp.int32, (16, 128), 0)
+    pick = (lane16 & 15) == row16
     sa[r] = jnp.zeros((8, 128), F32)
-    sa[r, 0:1, :] = moved[0:1, 0:128]
-    sa[r, 1:2, :] = moved[0:1, 128:256]
-    sa[r, 2:3, :] = moved[1:2, 0:128]
-    sa[r, 3:4, :] = moved[1:2, 128:256]
+    for i in range(2):
+        column = jnp.sum(acc[i], axis=1, keepdims=True)
+        sa[r, i : i + 1, :] = jnp.sum(jnp.where(pick, column, 0.0), axis=0, keepdims=True)
 
     def send_sa(j, carry):
         send(sa.at[r], sa.at[r], sa_tx, sa_rx, rep_dev(wrap(r + j, 16), t))
         return carry
 
     lax.fori_loop(1, 16, send_sa, 0)
+    ag4(0)
+    await_(sa.at[pl.ds(0, 15)], sa_rx)
+    sb[t] = jnp.zeros((8, 128), F32)
+    for i in range(2):
+        for h in range(2):
+            line = jnp.zeros((1, 128), F32)
+            for j in range(8):
+                line = line + jnp.where((lane16[0:1, :] >> 4) == j, sa[8 * h + j, i : i + 1, :], 0.0)
+            sb[t, 2 * i + h : 2 * i + h + 1, :] = line
+
+    def send_sb(j, carry):
+        send(sb.at[t], sb.at[t], sb_tx, sb_rx, rep_dev(r, wrap(t + j, 16)))
+        return carry
+
+    lax.fori_loop(1, 16, send_sb, 0)
+    flip(1)
     ag1(1)
     ag2(1)
-    await_(sa.at[pl.ds(0, 15)], sa_rx)
-    sb[t] = jnp.sum(sa[...], axis=0)
-
-    def send_sb(j, carry):
-        send(sb.at[t], sb.at[t], sb_tx, sb_rx, rep_dev(r, wrap(t + j, 16)))
-        return carry
-
-    lax.fori_loop(1, 16, send_sb, 0)
     ag3(1)
     await_(smr.at[pl.ds(0, 15)], sm_rx)
     await_(sb.at[pl.ds(0, 15)], sb_rx)
@@ -409,7 +446,7 @@
             count = count + jnp.sum(valid[p], axis=1, keepdims=True) * (1.0 / 16.0)
             weights.append(valid[p] / (1.0 + jnp.exp(margin)))
         halves.append((lens, firsts, seconds, inv, score, live, weights))
-    loss_ref[...] = jnp.broadcast_to(loss_sum / count, (8, 128))
+    misc_ref[4:8, :] = jnp.broadcast_to(loss_sum / count, (4, 128))
     factor = -scale[0] / count
     for h in range(2):
         lens, firsts, seconds, inv, score, live, weights = halves[h]
@@ -482,6 +519,8 @@
 
         lax.fori_loop(0, 4, group, 0)
 
+    for k in range(8):
+        await_(att.at[k, other], att_rxc.at[k])
     ag5(0)
     contract(0, True)
     ag5(1)
@@ -491,19 +530,18 @@
     def _():
         await_(gr.at[pl.ds(0, 15)], g_rx)
         await_(gr.at[pl.ds(0, 15)], g_tx)
-        await_(res.at[pl.ds(0, 15)], res_tx)
 
     @pl.when(jnp.logical_not(diag))
     def _():
         await_(gr, g_rx)
         await_(gr, g_tx)
-        await_(res, res_tx)
-        await_(vecr, vec_sem.at[0])
-
-    total = jnp.sum(gr[...], axis=0)
-    gg_ref[...] = total[0:4, :] * vec[4:8, :]
-    gh_ref[...] = total[0:4, :] * vec[0:4, :]
-
+
+    misc_ref[0:4, :] = jnp.sum(gr[...], axis=0)[0:4, :]
+
+    await_(rx.at[pl.ds(0, 15)], r1_tx)
+    await_(vall.at[pl.ds(0, 15)], vec_tx)
+    await_(zin.at[pl.ds(0, 7)], zin_tx.at[0])
+    await_(zin.at[pl.ds(0, 8)], zin_tx.at[1])
     await_(att.at[pl.ds(0, 7), 0], att_txz)
     await_(att.at[:, 0], att_txc)
     await_(smr.at[pl.ds(0, 15)], sm_tx)
@@ -516,40 +554,35 @@
 
 
 def shards(attn, out_weight, resid, norm_gain, head, lengths, pairs, pair_valid, loss_scale):
-    vec = jnp.concatenate([norm_gain, head]).astype(F32).reshape(8, 128)
-    small = jnp.concatenate([lengths, pairs[:, 0], pairs[:, 1], pair_valid])
-    small = jnp.pad(small, (0, 1024 - small.shape[0])).reshape(8, 128)
     vm = pltpu.VMEM
     dma = pltpu.SemaphoreType.DMA
     big = (4, 8, 2, 4, 16, 128)
     little = (4, 8, 2, 16, 128)
     vspec = pl.BlockSpec(memory_space=pltpu.VMEM)
     anyspec = pl.BlockSpec(memory_space=pl.ANY)
-    loss, out, gg, gh = pl.pallas_call(
+    smem = pl.BlockSpec(memory_space=pltpu.SMEM)
+    out, misc = pl.pallas_call(
         body,
         name="whole",
-        out_shape=(
-            jax.ShapeDtypeStruct((8, 128), F32),
-            jax.ShapeDtypeStruct((512, 512), F32),
-            jax.ShapeDtypeStruct((4, 128), F32),
-            jax.ShapeDtypeStruct((4, 128), F32),
-        ),
-        in_specs=[pl.BlockSpec(memory_space=pltpu.SMEM), anyspec, anyspec, anyspec, vspec, vspec],
-        out_specs=(vspec, vspec, vspec, vspec),
+        out_shape=(jax.ShapeDtypeStruct((512, 512), F32), jax.ShapeDtypeStruct((8, 128), F32)),
+        in_specs=[smem, smem, smem, smem, anyspec, anyspec, anyspec, vspec, vspec],
+        out_specs=(vspec, vspec),
         scratch_shapes=[
-            vm((8, 2, 256, 512), BF16), vm((512, 512), BF16), vm((256, 512), BF16), vm((16, 16, 512), BF16),
-            vm((8, 128), F32), vm((16, 8, 128), jnp.int32), vm((8, 2, 4, 4, 16, 512), F32),
+            vm((8, 2, 256, 512), BF16), vm((8, 1024, 512), BF16), vm((256, 512), BF16), vm((16, 16, 512), BF16),
+            vm((8, 2, 16, 512), BF16), vm((16, 16, 512), BF16), vm((8, 128), F32), vm((16, 8, 128), F32), vm((16, 4, 128), F32),
+            vm((2, 16, 128), F32), vm((16, 8, 128), jnp.int32), vm((8, 2, 4, 4, 16, 512), F32),
             vm(big, BF16), vm(big, BF16), vm(big, BF16), vm(big, BF16), vm(big, BF16), vm(big, BF16), vm(big, F32),
             vm(little, BF16), vm(little, BF16), vm(little, BF16), vm(little, BF16), vm(little, BF16), vm(little, BF16),
-            vm((16, 16, 512), F32), vm((4, 2, 128, 128), F32), vm((2, 16, 4, 128, 128), BF16), vm((4, 128, 128), F32),
-            vm((8, 256), F32), vm((16, 8, 128), F32), vm((16, 8, 128), F32), vm((16, 256), F32), vm((16, 256), F32), vm((16, 8, 256), F32),
+            vm((4, 2, 128, 128), F32), vm((2, 16, 4, 128, 128), BF16), vm((4, 128, 128), F32),
+            vm((16, 8, 128), F32), vm((16, 8, 128), F32), vm((16, 256), F32), vm((16, 256), F32), vm((16, 8, 256), F32),
             vm((8, 128), F32), vm((16, 8, 128), F32), vm((512, 512), BF16),
-            dma((3,)), dma, dma, dma((8, 2)), dma, dma, dma, dma((2,)), dma, dma,
+            dma((2,)), dma((8,)), dma, dma, dma((8, 4)), dma((8,)), dma, dma, dma((2,)), dma((2,)), dma, dma, dma, dma,
             dma((6, 4)), dma((6, 4, 8)), dma((4,)), dma((2, 4, 16)), dma, dma, dma, dma, dma, dma,
         ],
         compiler_params=pltpu.CompilerParams(collective_id=0, has_side_effects=True, vmem_limit_bytes=60 * 1024 * 1024),
-    )(loss_scale, attn, out_weight, resid, vec, small)
-    return (loss[0, 0:1], out, gg.reshape(512), gh.reshape(512))
+    )(loss_scale, lengths, pairs.T, pair_valid, attn, out_weight, resid, norm_gain, head)
+    g = misc[0:4].reshape(512)
+    return (misc[4, 0:1], out, g * head.astype(F32), g * norm_gain.astype(F32))
 
 
 def solution(mesh):

time: 127 us -> 87.5 us (0.69)
  Pallas kernels: 115 us -> 79.7 us
  local copies, waits for them, and re-layouts: 7.32 us -> 3.46 us
    pallas_call x1, Pallas kernels: 115 us -> 79.7 us  [shards(): pl.pallas_call(body, name='whole', out_shape=(jax.ShapeDtypeStruct((512,...]
    unnamed x3 -> x5, local copies, waits for them, and re-layouts: 4.78 us -> 2.27 us
    convert_element_type x1 -> x0, other arithmetic: 1.29 us -> none  [shards(): vec = jnp.concatenate([norm_gain, head]).astype(F32).reshape(8, 128)]
where the time goes in v3:
time: 87.5 us; the launch traced here: 85.8 us
  Pallas kernels  79.7 us (91%)
  local copies, waits for them, and re-layouts  3.46 us (4%)
  between operations  1.32 us (2%)
  other arithmetic  1.26 us (1%)
    pallas_call x1, Pallas kernels, shards(): pl.pallas_call(body, name='whole', out_shape=(jax.ShapeDtypeStruct((512,...  79.7 us
    unnamed x5, local copies, waits for them, and re-layouts  2.27 us

profile of v3, /device:TPU:4, one launch (start us, length us, event | category | flops | bytes accessed | tf_op | source)
XLA Modules:
  0.0 85.8 jit_solution(13029472692565777318)
XLA Ops:
  0.6 0.0 copy-start.1
  0.6 0.0 copy-start
  1.3 79.7 %whole.1 = (f32[512,512]{1,0:T(8,128)}, f32[8,128]{1,0:T(8,128)}) custom-call(f32[1]{0:T(128)S(6)} %copy.14.scale, s32[4]{0:T(128)} %lens_ref.1, s32[2,4]{1,0:T(2,128)} %bitcast.5, s32[4]{0:T(128)} %valid_ref.1, bf16[256,512]{1,0:T(8,128)(2,1)} %attn_hbm.1, bf16[8192,512]{1,0:T(8,128)(2,1)} %w_hbm.1, bf16[256,512]{1,0:T(8,128)(2,1)} %resid_hbm.1, ...), custom_call_target="tpu_custom_call" | custom-call | tf_op jit(solution)/shard_map/whole/pallas_call | solution.py:564
  81.0 1.2 %slice.6 = f32[1,1]{1,0:T(1,128)} slice(f32[8,128]{1,0:T(8,128)} %get-tuple-element.6), slice={[4:5], [0:1]} | slice | bytes 8 | tf_op jit(solution)/shard_map/slice | solution.py:585
  82.2 0.0 copy-done.1
  82.2 0.0 copy-done
  82.2 1.3 %bitcast_multiply_fusion = (f32[512]{0:T(512)}, f32[512]{0:T(512)}) fusion(bf16[512]{0:T(512)(128)(2,1)S(1)} %copy-done, f32[8,128]{1,0:T(8,128)} %get-tuple-element.6, bf16[512]{0:T(512)(128)(2,1)S(1)} %copy-done.1), kind=kLoop, calls=%fused_computation | loop fusion | flops 2048 | bytes 8192 | tf_op jit(solution)/shard_map/mul | solution.py:585
  83.5 2.3 %copy.15 = f32[512,512]{1,0:T(8,128)} copy(f32[512,512]{1,0:T(8,128)} %get-tuple-element.15) | data formatting | bytes 2097152
Async XLA Ops:
  0.6 81.6 %copy-start.1 = (bf16[512]{0:T(512)(128)(2,1)S(1)}, bf16[512]{0:T(512)(128)(2,1)}, u32[]{:S(2)}) copy-start(bf16[512]{0:T(512)(128)(2,1)} %head_ref.1) | copy-start | bytes 3076
  0.6 81.6 %copy-start = (bf16[512]{0:T(512)(128)(2,1)S(1)}, bf16[512]{0:T(512)(128)(2,1)}, u32[]{:S(2)}) copy-start(bf16[512]{0:T(512)(128)(2,1)} %gain_ref.1) | copy-start | bytes 3076

commit v4 on v3

--- a/solution.py
+++ b/solution.py
@@ -18,9 +18,9 @@
 
 
 def body(scale, lens_ref, pairs_ref, valid_ref, attn_hbm, w_hbm, resid_hbm, gain_ref, head_ref, out_ref, misc_ref,
-         att, wbuf, resbuf, rx, zo, zin, vec, vall, hgr, acc, smr, pf, m1s, m2s, m3s, m1r, m2r, m3r, s1f,
-         n1s, n2s, n3s, n1r, n2r, n3r, zt, za, hgc, sa, sb, ks, cs, kc, gmine, gr, dt,
-         loc_sem, w_sem, att_txz, att_txc, att_rx, att_rxc, r1_tx, r1_rx, zin_tx, zin_rx, vec_tx, vec_rx, sm_tx, sm_rx,
+         att, wbuf, resbuf, rx, zo, zin, zl, zlin, vec, vall, hgr, acc, smr, pf, m1s, m2s, m3s, m1r, m2r, m3r, s1f,
+         n1s, n2s, n3s, n1r, n2r, n3r, za, hgc, sa, sb, ks, cs, kc, gmine, gr, dt,
+         loc_sem, w_sem, att_txz, att_txc, att_rx, att_rxc, r1_tx, r1_rx, zin_tx, zin_rx, zl_tx, zl_rx, vec_tx, vec_rx, sm_tx, sm_rx,
          rs_tx, rs_rx, ag_tx, ag_rx, sa_tx, sa_rx, sb_tx, sb_rx, g_tx, g_rx):
     zc, core, x, y = (lax.axis_index(n) for n in ("z", "c", "x", "y"))
     r = zc * 2 + core
@@ -43,8 +43,12 @@
     load_r = pltpu.make_async_copy(resid_hbm, resbuf, loc_sem.at[1])
     load_a.start()
 
+    def place(k):
+        return 7 - (4 * lax.rem(k // 2, 2) + 2 * (k // 4) + lax.rem(k, 2))
+
     def offset(k):
-        return ((k + 1) // 2) * (2 * lax.rem(k, 2) - 1)
+        m = place(k)
+        return ((m + 1) // 2) * (2 * lax.rem(m, 2) - 1)
 
     def aim(k):
         return wrap(zc - offset(k), 8)
@@ -78,9 +82,17 @@
         return carry
 
     lax.fori_loop(0, 16, greet2, 0)
+    load_a.wait()
+
+    def multiply(k):
+        await_(wbuf.at[k], w_sem.at[k])
+        prod = lax.dot_general(att[0, core], wbuf[k], (((1,), (1,)), ((), ())), preferred_element_type=F32)
+        pf[k, 0] = prod[:, 0:512].reshape(4, 4, 16, 512)
+        pf[k, 1] = prod[:, 512:1024].reshape(4, 4, 16, 512)
+
+    multiply(0)
     pl.semaphore_wait(barrier, jnp.where(diag, 60, 62))
 
-    load_a.wait()
     def rows_of(j):
         return pl.ds(pl.multiple_of(j * 64, 64), 64)
 
@@ -91,12 +103,12 @@
         return att.at[k, core, rows_of(j)]
 
     def send_own(j, carry):
-        send(up(0, j), up(1, j), att_txz, att_rx.at[1, j], {"z": zm})
-        send(down(0, j), down(2, j), att_txz, att_rx.at[2, j], {"z": zp})
+        send(up(0, j), up(1, j), att_txz, att_rx.at[j], {"z": zm})
+        send(down(0, j), down(2, j), att_txz, att_rx.at[j], {"z": zp})
         return carry
 
     lax.fori_loop(0, 4, send_own, 0)
-    send(att.at[0, core], att.at[0, core], att_txc, att_rxc.at[0], {"c": other})
+    send(att.at[0, core], att.at[0, core], att_txc, att_rxc.at[1], {"c": other})
 
     def spread():
         lane8 = lax.broadcasted_iota(jnp.int32, (8, 128), 1)
@@ -114,6 +126,7 @@
         rx[t] = resbuf[pl.ds(pl.multiple_of(t * 16, 16), 16), :]
         acc[...] = jnp.zeros((2, 16, 128), F32)
 
+    def pieces(n):
         def one(j, carry):
             tt = wrap(t + j, 16)
             rows = pl.ds(pl.multiple_of(tt * 16, 16), 16)
@@ -122,7 +135,7 @@
             send(resbuf.at[rows, :], rx.at[t], r1_tx, r1_rx, rep_dev(r, tt))
             return carry
 
-        lax.fori_loop(1, 16, one, 0)
+        lax.fori_loop(3 * n - 2, 3 * n + 1, one, 0)
 
     def gathered():
         await_(vall.at[pl.ds(0, 15)], vec_rx)
@@ -156,167 +169,166 @@
         return a * 4 + b if g["q"] < 2 else b * 4 + a
 
     def ring(n):
+        n = jnp.int32(n)
         d, j = n // 4 + 1, lax.rem(n, 4)
         kp, km = 2 * d - 1, 2 * d
-
-        @pl.when(n < 8)
-        def _():
-            await_(up(kp, j), att_rx.at[kp, j])
-            send(up(kp, j), up(kp + 2, j), att_txz, att_rx.at[kp + 2, j], {"z": zm})
-            await_(down(km, j), att_rx.at[km, j])
-            send(down(km, j), down(km + 2, j), att_txz, att_rx.at[km + 2, j], {"z": zp})
-
-        @pl.when((n >= 8) & (n < 12))
-        def _():
-            await_(up(5, j), att_rx.at[5, j])
-
-            @pl.when(j < 2)
-            def _():
-                send(up(5, j), up(7, j), att_txz, att_rx.at[7, j], {"z": zm})
-
-            await_(down(6, j), att_rx.at[6, j])
-
-            @pl.when(j < 2)
-            def _():
-                send(down(6, j), down(7, j), att_txz, att_rx.at[7, j + 2], {"z": zp})
+        await_(att.at[0, core, pl.ds(0, 128)], att_rx.at[n])
+
+        @pl.when(n < 10)
+        def _():
+            send(up(kp, j), up(jnp.minimum(kp + 2, 7), j), att_txz, att_rx.at[n + 4], {"z": zm})
+            send(down(km, j), down(jnp.minimum(km + 2, 7), j), att_txz, att_rx.at[n + 4], {"z": zp})
 
         @pl.when((j == 3) & (n < 12))
         def _():
-            send(att.at[kp, core], att.at[kp, core], att_txc, att_rxc.at[kp], {"c": other})
-            send(att.at[km, core], att.at[km, core], att_txc, att_rxc.at[km], {"c": other})
-
-        @pl.when(n >= 12)
-        def _():
-            await_(up(7, j), att_rx.at[7, j])
-            await_(down(7, j), att_rx.at[7, j + 2])
-
-            @pl.when(j == 1)
-            def _():
-                send(att.at[7, core], att.at[7, core], att_txc, att_rxc.at[7], {"c": other})
+            h = jnp.where((kp == 3) | (kp == 7), 0, 1)
+            send(att.at[kp, core], att.at[kp, core], att_txc, att_rxc.at[h], {"c": other})
+            h = jnp.where((km == 2) | (km == 6), 0, 1)
+            send(att.at[km, core], att.at[km, core], att_txc, att_rxc.at[h], {"c": other})
+
+        @pl.when(n == 13)
+        def _():
+            send(att.at[7, core], att.at[7, core], att_txc, att_rxc.at[0], {"c": other})
 
     def step_a(k):
-        await_(wbuf.at[k], w_sem.at[k])
-        prod = lax.dot_general(att[0, core], wbuf[k], (((1,), (1,)), ((), ())), preferred_element_type=F32)
-        pf[k, 0] = prod[:, 0:512].reshape(4, 4, 16, 512)
-        pf[k, 1] = prod[:, 512:1024].reshape(4, 4, 16, 512)
+        @pl.when(k > 0)
+        def _():
+            multiply(k)
+
         for g in quarters:
             q = g["q"]
             m1s[q, k] = chunk(k, g, g["af"]).astype(BF16)
-            send(m1s.at[q, k], m1r.at[q, k], rs_tx.at[0, q], rs_rx.at[0, q, k], g["dan"])
+            send(m1s.at[q, k], m1r.at[q, k], rs_tx.at[0], rs_rx.at[0, k], g["dan"])
         for g in quarters:
             q = g["q"]
             m3s[q, k] = chunk(k, g, g["ao"]).astype(BF16)
-            send(m3s.at[q, k], m3r.at[q, k], rs_tx.at[1, q], rs_rx.at[1, q, k], g["dao"])
+            send(m3s.at[q, k], m3r.at[q, k], rs_tx.at[1], rs_rx.at[1, k], g["dao"])
 
     def step_b(k):
+        await_(m1r.at[:, k], rs_rx.at[0, k])
         for g in quarters:
             q = g["q"]
-            await_(m1r.at[q, k], rs_rx.at[0, q, k])
             m2s[q, k] = (chunk(k, g, g["an"]) + m1r[q, k].astype(F32)).astype(BF16)
-            send(m2s.at[q, k], m2r.at[q, k], rs_tx.at[2, q], rs_rx.at[2, q, k], g["dan"])
+            send(m2s.at[q, k], m2r.at[q, k], rs_tx.at[2], rs_rx.at[2, k], g["dan"])
 
     def step_c(k):
+        await_(m3r.at[:, k], rs_rx.at[1, k])
+        await_(m2r.at[:, k], rs_rx.at[2, k])
         for g in quarters:
             q = g["q"]
-            await_(m3r.at[q, k], rs_rx.at[1, q, k])
-            await_(m2r.at[q, k], rs_rx.at[2, q, k])
             s1f[q, k] = chunk(k, g, g["a0"]) + m2r[q, k].astype(F32) + m3r[q, k].astype(F32)
             n1s[q, k] = s1f[q, k, :, pl.ds(g["bf"], 1)].reshape(2, 16, 128).astype(BF16)
-            send(n1s.at[q, k], n1r.at[q, k], rs_tx.at[3, q], rs_rx.at[3, q, k], g["dbn"])
+            send(n1s.at[q, k], n1r.at[q, k], rs_tx.at[3], rs_rx.at[3, k], g["dbn"])
             n3s[q, k] = s1f[q, k, :, pl.ds(g["bo"], 1)].reshape(2, 16, 128).astype(BF16)
-            send(n3s.at[q, k], n3r.at[q, k], rs_tx.at[4, q], rs_rx.at[4, q, k], g["dbo"])
+            send(n3s.at[q, k], n3r.at[q, k], rs_tx.at[4], rs_rx.at[4, k], g["dbo"])
 
     def step_d(k):
+        await_(n1r.at[:, k], rs_rx.at[3, k])
         for g in quarters:
             q = g["q"]
-            await_(n1r.at[q, k], rs_rx.at[3, q, k])
             n2s[q, k] = (s1f[q, k, :, pl.ds(g["bn"], 1)].reshape(2, 16, 128) + n1r[q, k].astype(F32)).astype(BF16)
-            send(n2s.at[q, k], n2r.at[q, k], rs_tx.at[5, q], rs_rx.at[5, q, k], g["dbn"])
+            send(n2s.at[q, k], n2r.at[q, k], rs_tx.at[5], rs_rx.at[5, k], g["dbn"])
 
     def step_e(k):
         dz = aim(k)
         sq = jnp.zeros((16, 128), F32)
         dot = jnp.zeros((16, 128), F32)
+        await_(n2r.at[:, k], rs_rx.at[5, k])
+        await_(n3r.at[:, k], rs_rx.at[4, k])
         for g in quarters:
             q = g["q"]
-            await_(n2r.at[q, k], rs_rx.at[5, q, k])
-            await_(n3r.at[q, k], rs_rx.at[4, q, k])
             total = s1f[q, k, :, pl.ds(g["b0"], 1)].reshape(2, 16, 128) + n2r[q, k].astype(F32) + n3r[q, k].astype(F32)
             total = total + rx[pl.ds(2 * dz, 2), :, g["lanes"]].astype(F32)
             for cc in range(2):
                 sq = sq + total[cc] * total[cc]
                 dot = dot + total[cc] * hgr[2 * dz + cc, q : q + 1, :]
-            zo[k, :, :, g["lanes"]] = total.astype(BF16)
+            high = total.astype(BF16)
+            zo[k, :, :, g["lanes"]] = high
+            zl[k, :, :, g["lanes"]] = (total - high.astype(F32)).astype(BF16)
         acc[0] += sq
         acc[1] += dot
         h = k // 4
 
-        @pl.when(k == 0)
-        def _():
-            zin[core] = zo[0, core]
-
-        @pl.when(k > 0)
+        @pl.when(k == 7)
+        def _():
+            zin[14 + core] = zo[7, core]
+
+        @pl.when(k < 7)
         def _():
             send(zo.at[k, core], zin.at[2 * k + core], zin_tx.at[h], zin_rx.at[h], {"z": dz})
 
         send(zo.at[k, other], zin.at[2 * k + core], zin_tx.at[h], zin_rx.at[h], {"z": dz, "c": other})
 
+    def send_low(k, carry):
+        dz = aim(k)
+
+        @pl.when(k == 7)
+        def _():
+            zlin[14 + core] = zl[7, core]
+
+        @pl.when(k < 7)
+        def _():
+            send(zl.at[k, core], zlin.at[2 * k + core], zl_tx, zl_rx, {"z": dz})
+
+        send(zl.at[k, other], zlin.at[2 * k + core], zl_tx, zl_rx, {"z": dz, "c": other})
+        return carry
+
     def flip(h):
-        await_(zin.at[pl.ds(0, 7 + h)], zin_rx.at[h])
+        await_(zin.at[pl.ds(0, 8 - h)], zin_rx.at[h])
         v = zin[8 * h : 8 * h + 8].reshape(128, 512).astype(F32)
         for q in range(4):
-            turned = v[:, q * 128 : (q + 1) * 128].T
-            zt[q, h] = turned
-            za[h, t, q] = turned.astype(BF16)
-
-    def gsend(h, g, a, b, dev):
+            za[h, t, q] = v[:, q * 128 : (q + 1) * 128].T.astype(BF16)
+
+    def gsend(h, g, a, b, dev, event):
         q = g["q"]
-        tt = tcol(g, a, b)
-        send(za.at[h, tt, q], za.at[h, tt, q], ag_tx.at[q], ag_rx.at[h, q, tt], dev)
-
-    def gwait(h, g, a, b):
-        q = g["q"]
-        tt = tcol(g, a, b)
-        await_(za.at[h, tt, q], ag_rx.at[h, q, tt])
+        tt = tcol(g, g[a], g[b])
+        send(za.at[h, tt, q], za.at[h, tt, q], ag_tx, ag_rx.at[h, event], g[dev])
+
+    def gwait(h, event):
+        await_(za.at[h, 0], ag_rx.at[h, event])
 
     def ag1(h):
         for g in quarters:
-            gsend(h, g, g["a0"], g["b0"], g["dan"])
-            gsend(h, g, g["a0"], g["b0"], g["dao"])
-        for g in quarters:
-            gsend(h, g, g["a0"], g["b0"], g["dbn"])
-            gsend(h, g, g["a0"], g["b0"], g["dbo"])
+            gsend(h, g, "a0", "b0", "dan", 0)
+            gsend(h, g, "a0", "b0", "dao", 1)
+        for g in quarters:
+            gsend(h, g, "a0", "b0", "dbn", 3)
+            gsend(h, g, "a0", "b0", "dbo", 7)
 
     def ag2(h):
-        for g in quarters:
-            gwait(h, g, g["ao"], g["b0"])
-            gsend(h, g, g["ao"], g["b0"], g["dan"])
-        for g in quarters:
-            gsend(h, g, g["ao"], g["b0"], g["dbn"])
-            gsend(h, g, g["ao"], g["b0"], g["dbo"])
-            gwait(h, g, g["an"], g["b0"])
-            gsend(h, g, g["an"], g["b0"], g["dbn"])
-            gsend(h, g, g["an"], g["b0"], g["dbo"])
+        gwait(h, 0)
+        for g in quarters:
+            gsend(h, g, "ao", "b0", "dan", 2)
+        for g in quarters:
+            gsend(h, g, "ao", "b0", "dbn", 4)
+        gwait(h, 1)
+        for g in quarters:
+            gsend(h, g, "an", "b0", "dbn", 5)
+        for g in quarters:
+            gsend(h, g, "ao", "b0", "dbo", 7)
+            gsend(h, g, "an", "b0", "dbo", 7)
 
     def ag3(h):
-        for g in quarters:
-            gwait(h, g, g["a0"], g["bo"])
-            gsend(h, g, g["a0"], g["bo"], g["dbn"])
-            gwait(h, g, g["af"], g["b0"])
-            gsend(h, g, g["af"], g["b0"], g["dbn"])
-            gsend(h, g, g["af"], g["b0"], g["dbo"])
+        gwait(h, 3)
+        for g in quarters:
+            gsend(h, g, "a0", "bo", "dbn", 7)
+        gwait(h, 2)
+        for g in quarters:
+            gsend(h, g, "af", "b0", "dbn", 6)
+        for g in quarters:
+            gsend(h, g, "af", "b0", "dbo", 7)
+
+    def ag4part(h, i):
+        gwait(h, 4 + i)
+        for g in quarters:
+            gsend(h, g, ("ao", "an", "af")[i], "bo", "dbn", 7)
 
     def ag4(h):
-        for g in quarters:
-            for a in ("ao", "an", "af"):
-                gwait(h, g, g[a], g["bo"])
-                gsend(h, g, g[a], g["bo"], g["dbn"])
+        for i in range(3):
+            ag4part(h, i)
 
     def ag5(h):
-        for g in quarters:
-            for a in ("a0", "ao", "an", "af"):
-                gwait(h, g, g[a], g["bn"])
-                gwait(h, g, g[a], g["bf"])
+        await_(za.at[h, pl.ds(0, 8)], ag_rx.at[h, 7])
 
     def on(n, parity, first, fn):
         k = (n - first) // 2
@@ -336,26 +348,22 @@
         on(n, 1, 3, step_b)
         on(n, 0, 0, step_a)
 
-        @pl.when(n == 1)
+        @pl.when(n == 0)
         def _():
             spread()
 
-        @pl.when((n >= 7) & (n < 21))
-        def _():
-            ring(n - 7)
+        @pl.when((n >= 1) & (n < 6))
+        def _():
+            pieces(n)
+
+        @pl.when((n >= 5) & (lax.rem(n, 2) == 1))
+        def _():
+            ring((n - 5) // 2)
 
         @pl.when(n == 21)
         def _():
             flip(0)
             ag1(0)
-
-        @pl.when(n == 24)
-        def _():
-            ag2(0)
-
-        @pl.when(n == 25)
-        def _():
-            ag3(0)
 
         return carry
 
@@ -364,7 +372,8 @@
     def absolute(lane):
         slot = lane >> 4
         k = slot >> 1
-        off = ((k + 1) >> 1) * (2 * (k & 1) - 1)
+        m = 7 - (4 * ((k >> 1) & 1) + 2 * (k >> 2) + (k & 1))
+        off = ((m + 1) >> 1) * (2 * (m & 1) - 1)
         return ((((zc + off + 8) & 7) * 2 + (slot & 1)) << 4) + (lane & 15)
 
     rows256 = lax.broadcasted_iota(jnp.int32, (256, 256), 0)
@@ -382,7 +391,11 @@
         return carry
 
     lax.fori_loop(1, 16, send_sa, 0)
-    ag4(0)
+    lax.fori_loop(0, 8, send_low, 0)
+    ag2(0)
+    flip(1)
+    ag1(1)
+    ag3(0)
     await_(sa.at[pl.ds(0, 15)], sa_rx)
     sb[t] = jnp.zeros((8, 128), F32)
     for i in range(2):
@@ -397,10 +410,14 @@
         return carry
 
     lax.fori_loop(1, 16, send_sb, 0)
-    flip(1)
-    ag1(1)
     ag2(1)
+    ring(11)
+    ag4(0)
+    ring(12)
+    ring(13)
     ag3(1)
+    ag4part(1, 0)
+    ag4part(1, 1)
     await_(smr.at[pl.ds(0, 15)], sm_rx)
     await_(sb.at[pl.ds(0, 15)], sb_rx)
 
@@ -467,11 +484,16 @@
         kc[i, 0:1, :] = kslot[i : i + 1, :]
         kc[i, 1:2, :] = cslot[i : i + 1, :]
 
+    await_(zlin.at[pl.ds(0, 15)], zl_rx)
     krow = [kc[t, 0:1, 0:128], kc[t, 0:1, 128:256]]
     gsum = jnp.zeros((8, 128), F32)
     for q in range(4):
-        prod = zt[q, 0] * krow[0] + zt[q, 1] * krow[1]
-        row = jnp.sum(prod.T, axis=0, keepdims=True)
+        row = jnp.zeros((1, 128), F32)
+        for h in range(2):
+            column = jnp.broadcast_to(krow[h], (128, 128)).T
+            full = zin[8 * h : 8 * h + 8, :, q * 128 : (q + 1) * 128].astype(F32)
+            full = full + zlin[8 * h : 8 * h + 8, :, q * 128 : (q + 1) * 128].astype(F32)
+            row = row + jnp.sum(full.reshape(128, 128) * column, axis=0, keepdims=True)
         gsum = gsum + jnp.where(eight == q, row, 0.0)
     gmine[...] = gsum
 
@@ -489,10 +511,14 @@
         return carry
 
     lax.fori_loop(0, 16, send_g, 0)
-    ag4(1)
 
     def contract(h, first):
         def group(gi, carry):
+            if first:
+                @pl.when(gi == 1)
+                def _():
+                    ag4part(1, 2)
+
             parts = []
             for j in range(4):
                 tt = gi * 4 + j
@@ -501,7 +527,9 @@
                 for q in range(4):
                     val = hgc[q] * k1 - za[h, tt, q].astype(F32) * c1
                     dt[q * 128 : (q + 1) * 128, j * 128 : (j + 1) * 128] = val.astype(BF16)
-                parts.append(att[4 * h : 4 * h + 4, :, pl.ds(pl.multiple_of(tt * 16, 16), 16), :].reshape(128, 512))
+                rows = pl.ds(pl.multiple_of(tt * 16, 16), 16)
+                for k in range(4 * h, 4 * h + 4):
+                    parts.append(att[7 - (4 * (k // 2 % 2) + 2 * (k // 4) + k % 2), :, rows, :].reshape(32, 512))
             rhs = jnp.concatenate(parts, axis=0)
             prod = jnp.dot(dt[...], rhs, preferred_element_type=F32)
 
@@ -519,8 +547,8 @@
 
         lax.fori_loop(0, 4, group, 0)
 
-    for k in range(8):
-        await_(att.at[k, other], att_rxc.at[k])
+    await_(att.at[pl.ds(0, 4), 0], att_rxc.at[0])
+    await_(att.at[pl.ds(0, 4), 0], att_rxc.at[1])
     ag5(0)
     contract(0, True)
     ag5(1)
@@ -540,17 +568,17 @@
 
     await_(rx.at[pl.ds(0, 15)], r1_tx)
     await_(vall.at[pl.ds(0, 15)], vec_tx)
-    await_(zin.at[pl.ds(0, 7)], zin_tx.at[0])
-    await_(zin.at[pl.ds(0, 8)], zin_tx.at[1])
+    await_(zin.at[pl.ds(0, 8)], zin_tx.at[0])
+    await_(zlin.at[pl.ds(0, 15)], zl_tx)
+    await_(zin.at[pl.ds(0, 7)], zin_tx.at[1])
     await_(att.at[pl.ds(0, 7), 0], att_txz)
     await_(att.at[:, 0], att_txc)
     await_(smr.at[pl.ds(0, 15)], sm_tx)
     await_(sa.at[pl.ds(0, 15)], sa_tx)
     await_(sb.at[pl.ds(0, 15)], sb_tx)
-    for q in range(4):
-        for i, buf in enumerate((m1s, m3s, m2s, n1s, n3s, n2s)):
-            await_(buf.at[q], rs_tx.at[i, q])
-        await_(za.at[:, pl.ds(0, 15), q], ag_tx.at[q])
+    for i, buf in enumerate((m1s, m3s, m2s, n1s, n3s, n2s)):
+        await_(buf, rs_tx.at[i])
+    await_(za.at[:, pl.ds(0, 15)], ag_tx)
 
 
 def shards(attn, out_weight, resid, norm_gain, head, lengths, pairs, pair_valid, loss_scale):
@@ -559,7 +587,7 @@
     big = (4, 8, 2, 4, 16, 128)
     little = (4, 8, 2, 16, 128)
     vspec = pl.BlockSpec(memory_space=pltpu.VMEM)
-    anyspec = pl.BlockSpec(memory_space=pl.ANY)
+    anyspec = pl.BlockSpec(memory_space=pltpu.HBM)
     smem = pl.BlockSpec(memory_space=pltpu.SMEM)
     out, misc = pl.pallas_call(
         body,
@@ -569,15 +597,15 @@
         out_specs=(vspec, vspec),
         scratch_shapes=[
             vm((8, 2, 256, 512), BF16), vm((8, 1024, 512), BF16), vm((256, 512), BF16), vm((16, 16, 512), BF16),
-            vm((8, 2, 16, 512), BF16), vm((16, 16, 512), BF16), vm((8, 128), F32), vm((16, 8, 128), F32), vm((16, 4, 128), F32),
+            vm((8, 2, 16, 512), BF16), vm((16, 16, 512), BF16), vm((8, 2, 16, 512), BF16), vm((16, 16, 512), BF16), vm((8, 128), F32), vm((16, 8, 128), F32), vm((16, 4, 128), F32),
             vm((2, 16, 128), F32), vm((16, 8, 128), jnp.int32), vm((8, 2, 4, 4, 16, 512), F32),
             vm(big, BF16), vm(big, BF16), vm(big, BF16), vm(big, BF16), vm(big, BF16), vm(big, BF16), vm(big, F32),
             vm(little, BF16), vm(little, BF16), vm(little, BF16), vm(little, BF16), vm(little, BF16), vm(little, BF16),
-            vm((4, 2, 128, 128), F32), vm((2, 16, 4, 128, 128), BF16), vm((4, 128, 128), F32),
+            vm((2, 16, 4, 128, 128), BF16), vm((4, 128, 128), F32),
             vm((16, 8, 128), F32), vm((16, 8, 128), F32), vm((16, 256), F32), vm((16, 256), F32), vm((16, 8, 256), F32),
             vm((8, 128), F32), vm((16, 8, 128), F32), vm((512, 512), BF16),
-            dma((2,)), dma((8,)), dma, dma, dma((8, 4)), dma((8,)), dma, dma, dma((2,)), dma((2,)), dma, dma, dma, dma,
-            dma((6, 4)), dma((6, 4, 8)), dma((4,)), dma((2, 4, 16)), dma, dma, dma, dma, dma, dma,
+            dma((2,)), dma((8,)), dma, dma, dma((14,)), dma((2,)), dma, dma, dma((2,)), dma((2,)), dma, dma, dma, dma, dma, dma,
+            dma((6,)), dma((6, 8)), dma, dma((2, 8)), dma, dma, dma, dma, dma, dma,
         ],
         compiler_params=pltpu.CompilerParams(collective_id=0, has_side_effects=True, vmem_limit_bytes=60 * 1024 * 1024),
     )(loss_scale, lengths, pairs.T, pair_valid, attn, out_weight, resid, norm_gain, head)

time: 87.5 us -> 82.6 us (0.944); the launches traced: 85.8 us -> 82.4 us
  Pallas kernels: 79.7 us -> 76.4 us
    pallas_call x1, Pallas kernels: 79.7 us -> 76.4 us  [shards(): pl.pallas_call(body, name='whole', out_shape=(jax.ShapeDtypeStruct((512,...]
where the time goes in v4:
time: 82.6 us; the launch traced here: 82.4 us
  Pallas kernels  76.4 us (92%)
  local copies, waits for them, and re-layouts  3.46 us (4%)
  between operations  1.32 us (2%)
  other arithmetic  1.26 us (2%)
    pallas_call x1, Pallas kernels, shards(): pl.pallas_call(body, name='whole', out_shape=(jax.ShapeDtypeStruct((512,...  76.4 us
    unnamed x5, local copies, waits for them, and re-layouts  2.27 us

profile of v4, /device:TPU:4, one launch (start us, length us, event | category | flops | bytes accessed | tf_op | source)
XLA Modules:
  0.0 82.4 jit_solution(16938069508379284269)
XLA Ops:
  0.6 0.0 copy-start.1
  0.6 0.0 copy-start
  1.3 76.4 %whole.1 = (f32[512,512]{1,0:T(8,128)}, f32[8,128]{1,0:T(8,128)}) custom-call(f32[1]{0:T(128)S(6)} %copy.14.scale, s32[4]{0:T(128)} %lens_ref.1, s32[2,4]{1,0:T(2,128)} %bitcast.5, s32[4]{0:T(128)} %valid_ref.1, bf16[256,512]{1,0:T(8,128)(2,1)} %attn_hbm.1, bf16[8192,512]{1,0:T(8,128)(2,1)} %w_hbm.1, bf16[256,512]{1,0:T(8,128)(2,1)} %resid_hbm.1, ...), custom_call_target="tpu_custom_call" | custom-call | tf_op jit(solution)/shard_map/whole/pallas_call | solution.py:592
  77.7 1.2 %slice.6 = f32[1,1]{1,0:T(1,128)} slice(f32[8,128]{1,0:T(8,128)} %get-tuple-element.6), slice={[4:5], [0:1]} | slice | bytes 8 | tf_op jit(solution)/shard_map/slice | solution.py:613
  78.9 0.0 copy-done.1
  78.9 0.0 copy-done
  78.9 1.3 %bitcast_multiply_fusion = (f32[512]{0:T(512)}, f32[512]{0:T(512)}) fusion(bf16[512]{0:T(512)(128)(2,1)S(1)} %copy-done, f32[8,128]{1,0:T(8,128)} %get-tuple-element.6, bf16[512]{0:T(512)(128)(2,1)S(1)} %copy-done.1), kind=kLoop, calls=%fused_computation | loop fusion | flops 2048 | bytes 8192 | tf_op jit(solution)/shard_map/mul | solution.py:613
  80.1 2.3 %copy.15 = f32[512,512]{1,0:T(8,128)} copy(f32[512,512]{1,0:T(8,128)} %get-tuple-element.15) | data formatting | bytes 2097152
Async XLA Ops:
  0.6 78.2 %copy-start.1 = (bf16[512]{0:T(512)(128)(2,1)S(1)}, bf16[512]{0:T(512)(128)(2,1)}, u32[]{:S(2)}) copy-start(bf16[512]{0:T(512)(128)(2,1)} %head_ref.1) | copy-start | bytes 3076
  0.6 78.2 %copy-start = (bf16[512]{0:T(512)(128)(2,1)S(1)}, bf16[512]{0:T(512)(128)(2,1)}, u32[]{:S(2)}) copy-start(bf16[512]{0:T(512)(128)(2,1)} %gain_ref.1) | copy-start | bytes 3076

commit v5 on v4

--- a/solution.py
+++ b/solution.py
@@ -17,11 +17,11 @@
     return lax.rem(value + size, size)
 
 
-def body(scale, lens_ref, pairs_ref, valid_ref, attn_hbm, w_hbm, resid_hbm, gain_ref, head_ref, out_ref, misc_ref,
-         att, wbuf, resbuf, rx, zo, zin, zl, zlin, vec, vall, hgr, acc, smr, pf, m1s, m2s, m3s, m1r, m2r, m3r, s1f,
+def body(scale, lens_hbm, pairs_hbm, valid_hbm, attn_hbm, w_hbm, resid_hbm, gain_hbm, head_hbm, out_ref, misc_ref,
+         lens_ref, pairs_ref, valid_ref, gain_ref, head_ref, att, wbuf, resbuf, rx, zo, zin, zl, zlin, vec, vall, hgr, acc, hl, vsum, dd, smr, pf, m1s, m2s, m3s, m1r, m2r, m3r, s1f,
          n1s, n2s, n3s, n1r, n2r, n3r, za, hgc, sa, sb, ks, cs, kc, gmine, gr, dt,
-         loc_sem, w_sem, att_txz, att_txc, att_rx, att_rxc, r1_tx, r1_rx, zin_tx, zin_rx, zl_tx, zl_rx, vec_tx, vec_rx, sm_tx, sm_rx,
-         rs_tx, rs_rx, ag_tx, ag_rx, sa_tx, sa_rx, sb_tx, sb_rx, g_tx, g_rx):
+         loc_sem, small_sem, w_sem, att_txz, att_txc, att_rx, att_rxc, r1_tx, r1_rx, zin_tx, zin_rx, zl_tx, zl_rx, vec_tx, vec_rx, sm_tx, sm_rx,
+         rs_tx, rs_rx, ag_tx, ag_rx, sa_tx, sa_rx, sb_tx, sb_rx, g_tx, g_rx, dd_tx, dd_rx):
     zc, core, x, y = (lax.axis_index(n) for n in ("z", "c", "x", "y"))
     r = zc * 2 + core
     t = x * 4 + y
@@ -42,6 +42,12 @@
     load_a = pltpu.make_async_copy(attn_hbm, att.at[0, core], loc_sem.at[0])
     load_r = pltpu.make_async_copy(resid_hbm, resbuf, loc_sem.at[1])
     load_a.start()
+    loads = [
+        pltpu.make_async_copy(a, b, small_sem.at[i])
+        for i, (a, b) in enumerate((
+            (lens_hbm, lens_ref), (pairs_hbm, pairs_ref), (valid_hbm, valid_ref), (gain_hbm, gain_ref), (head_hbm, head_ref)
+        ))
+    ]
 
     def place(k):
         return 7 - (4 * lax.rem(k // 2, 2) + 2 * (k // 4) + lax.rem(k, 2))
@@ -58,8 +64,7 @@
         pltpu.make_async_copy(w_hbm.at[rows], wbuf.at[k], w_sem.at[k]).start()
         return carry
 
-    lax.fori_loop(0, 8, load_w, 0)
-    load_r.start()
+    load_w(0, 0)
 
     barrier = pltpu.get_barrier_semaphore()
 
@@ -82,6 +87,10 @@
         return carry
 
     lax.fori_loop(0, 16, greet2, 0)
+    lax.fori_loop(1, 8, load_w, 0)
+    load_r.start()
+    for load in loads:
+        load.start()
     load_a.wait()
 
     def multiply(k):
@@ -111,6 +120,8 @@
     send(att.at[0, core], att.at[0, core], att_txc, att_rxc.at[1], {"c": other})
 
     def spread():
+        for load in loads:
+            load.wait()
         lane8 = lax.broadcasted_iota(jnp.int32, (8, 128), 1)
         ints8 = jnp.zeros((8, 128), jnp.int32)
         for i in range(4):
@@ -124,7 +135,9 @@
         vall[t] = vec[...]
         load_r.wait()
         rx[t] = resbuf[pl.ds(pl.multiple_of(t * 16, 16), 16), :]
-        acc[...] = jnp.zeros((2, 16, 128), F32)
+        acc[...] = jnp.zeros((16, 128), F32)
+        hl[...] = jnp.zeros((8, 1024), F32)
+        vsum[...] = jnp.zeros((8, 512), F32)
 
     def pieces(n):
         def one(j, carry):
@@ -232,7 +245,6 @@
     def step_e(k):
         dz = aim(k)
         sq = jnp.zeros((16, 128), F32)
-        dot = jnp.zeros((16, 128), F32)
         await_(n2r.at[:, k], rs_rx.at[5, k])
         await_(n3r.at[:, k], rs_rx.at[4, k])
         for g in quarters:
@@ -241,12 +253,10 @@
             total = total + rx[pl.ds(2 * dz, 2), :, g["lanes"]].astype(F32)
             for cc in range(2):
                 sq = sq + total[cc] * total[cc]
-                dot = dot + total[cc] * hgr[2 * dz + cc, q : q + 1, :]
             high = total.astype(BF16)
             zo[k, :, :, g["lanes"]] = high
             zl[k, :, :, g["lanes"]] = (total - high.astype(F32)).astype(BF16)
-        acc[0] += sq
-        acc[1] += dot
+        acc[...] += sq
         h = k // 4
 
         @pl.when(k == 7)
@@ -258,6 +268,45 @@
             send(zo.at[k, core], zin.at[2 * k + core], zin_tx.at[h], zin_rx.at[h], {"z": dz})
 
         send(zo.at[k, other], zin.at[2 * k + core], zin_tx.at[h], zin_rx.at[h], {"z": dz, "c": other})
+
+    def halves_of(row):
+        high = row.astype(BF16).astype(F32)
+        return high, row - high
+
+    def project_head(k):
+        for cc in range(2):
+            for q in range(4):
+                at = slice((cc * 4 + q) * 128, (cc * 4 + q + 1) * 128)
+                high, low = halves_of(hgr[2 * aim(k) + cc, q : q + 1, :])
+                hl[0:1, at] = high
+                hl[1:2, at] = low
+        vsum[...] += jnp.dot(hl[...].astype(BF16), wbuf[k], preferred_element_type=F32)
+
+    def head_dots():
+        high, rest = halves_of(vsum[0:1, :] + vsum[1:2, :])
+        middle, low = halves_of(rest)
+        hl[0:1, 0:512] = high
+        hl[1:2, 0:512] = middle
+        hl[2:3, 0:512] = low
+        for q in range(4):
+            at = slice(512 + q * 128, 640 + q * 128)
+            high, low = halves_of(hgr[t, q : q + 1, :])
+            hl[0:1, at] = high
+            hl[1:2, at] = low
+        rows = hl[...].astype(BF16)
+        along = (((1,), (1,)), ((), ()))
+        a = lax.dot_general(rows[:, 0:512], att[0, core], along, preferred_element_type=F32)
+        b = lax.dot_general(rows[:, 512:1024], resbuf[...], along, preferred_element_type=F32)
+        line = a[0:1] + a[1:2] + a[2:3] + b[0:1] + b[1:2]
+        dd[t] = jnp.zeros((8, 128), F32)
+        dd[t, 0:1, :] = line[:, 0:128]
+        dd[t, 1:2, :] = line[:, 128:256]
+
+        def one(j, carry):
+            send(dd.at[t], dd.at[t], dd_tx, dd_rx, rep_dev(r, wrap(t + j, 16)))
+            return carry
+
+        lax.fori_loop(1, 16, one, 0)
 
     def send_low(k, carry):
         dz = aim(k)
@@ -359,6 +408,14 @@
         @pl.when((n >= 5) & (lax.rem(n, 2) == 1))
         def _():
             ring((n - 5) // 2)
+
+        @pl.when((n >= 13) & (n < 21))
+        def _():
+            project_head(n - 13)
+
+        @pl.when(n == 22)
+        def _():
+            head_dots()
 
         @pl.when(n == 21)
         def _():
@@ -382,9 +439,17 @@
     row16 = lax.broadcasted_iota(jnp.int32, (16, 128), 0)
     pick = (lane16 & 15) == row16
     sa[r] = jnp.zeros((8, 128), F32)
-    for i in range(2):
-        column = jnp.sum(acc[i], axis=1, keepdims=True)
-        sa[r, i : i + 1, :] = jnp.sum(jnp.where(pick, column, 0.0), axis=0, keepdims=True)
+    column = jnp.sum(acc[...], axis=1, keepdims=True)
+    sa[r, 0:1, :] = jnp.sum(jnp.where(pick, column, 0.0), axis=0, keepdims=True)
+    await_(dd.at[pl.ds(0, 15)], dd_rx)
+    dots = jnp.sum(dd[...], axis=0)
+    own_r = lax.broadcasted_iota(jnp.int32, (128, 128), 0)
+    own_c = lax.broadcasted_iota(jnp.int32, (128, 128), 1)
+    line = jnp.zeros((1, 128), F32)
+    for h in range(2):
+        own = ((own_r + 128 * h) == (t * 16 + (own_c & 15))).astype(F32)
+        line = line + jnp.dot(dots, own, precision=HIGH, preferred_element_type=F32)[h : h + 1, :]
+    sa[r, 1:2, :] = line
 
     def send_sa(j, carry):
         send(sa.at[r], sa.at[r], sa_tx, sa_rx, rep_dev(wrap(r + j, 16), t))
@@ -575,6 +640,7 @@
     await_(att.at[:, 0], att_txc)
     await_(smr.at[pl.ds(0, 15)], sm_tx)
     await_(sa.at[pl.ds(0, 15)], sa_tx)
+    await_(dd.at[pl.ds(0, 15)], dd_tx)
     await_(sb.at[pl.ds(0, 15)], sb_tx)
     for i, buf in enumerate((m1s, m3s, m2s, n1s, n3s, n2s)):
         await_(buf, rs_tx.at[i])
@@ -583,6 +649,7 @@
 
 def shards(attn, out_weight, resid, norm_gain, head, lengths, pairs, pair_valid, loss_scale):
     vm = pltpu.VMEM
+    stay = lambda a: pltpu.with_memory_space_constraint(a, pltpu.HBM)
     dma = pltpu.SemaphoreType.DMA
     big = (4, 8, 2, 4, 16, 128)
     little = (4, 8, 2, 16, 128)
@@ -593,22 +660,24 @@
         body,
         name="whole",
         out_shape=(jax.ShapeDtypeStruct((512, 512), F32), jax.ShapeDtypeStruct((8, 128), F32)),
-        in_specs=[smem, smem, smem, smem, anyspec, anyspec, anyspec, vspec, vspec],
+        in_specs=[smem] + [anyspec] * 8,
         out_specs=(vspec, vspec),
         scratch_shapes=[
+            pltpu.SMEM((4,), jnp.int32), pltpu.SMEM((2, 4), jnp.int32), pltpu.SMEM((4,), jnp.int32),
+            vm((512,), BF16), vm((512,), BF16),
             vm((8, 2, 256, 512), BF16), vm((8, 1024, 512), BF16), vm((256, 512), BF16), vm((16, 16, 512), BF16),
             vm((8, 2, 16, 512), BF16), vm((16, 16, 512), BF16), vm((8, 2, 16, 512), BF16), vm((16, 16, 512), BF16), vm((8, 128), F32), vm((16, 8, 128), F32), vm((16, 4, 128), F32),
-            vm((2, 16, 128), F32), vm((16, 8, 128), jnp.int32), vm((8, 2, 4, 4, 16, 512), F32),
+            vm((16, 128), F32), vm((8, 1024), F32), vm((8, 512), F32), vm((16, 8, 128), F32), vm((16, 8, 128), jnp.int32), vm((8, 2, 4, 4, 16, 512), F32),
             vm(big, BF16), vm(big, BF16), vm(big, BF16), vm(big, BF16), vm(big, BF16), vm(big, BF16), vm(big, F32),
             vm(little, BF16), vm(little, BF16), vm(little, BF16), vm(little, BF16), vm(little, BF16), vm(little, BF16),
             vm((2, 16, 4, 128, 128), BF16), vm((4, 128, 128), F32),
             vm((16, 8, 128), F32), vm((16, 8, 128), F32), vm((16, 256), F32), vm((16, 256), F32), vm((16, 8, 256), F32),
             vm((8, 128), F32), vm((16, 8, 128), F32), vm((512, 512), BF16),
-            dma((2,)), dma((8,)), dma, dma, dma((14,)), dma((2,)), dma, dma, dma((2,)), dma((2,)), dma, dma, dma, dma, dma, dma,
-            dma((6,)), dma((6, 8)), dma, dma((2, 8)), dma, dma, dma, dma, dma, dma,
+            dma((2,)), dma((5,)), dma((8,)), dma, dma, dma((14,)), dma((2,)), dma, dma, dma((2,)), dma((2,)), dma, dma, dma, dma, dma, dma,
+            dma((6,)), dma((6, 8)), dma, dma((2, 8)), dma, dma, dma, dma, dma, dma, dma, dma,
         ],
-        compiler_params=pltpu.CompilerParams(collective_id=0, has_side_effects=True, vmem_limit_bytes=60 * 1024 * 1024),
-    )(loss_scale, lengths, pairs.T, pair_valid, attn, out_weight, resid, norm_gain, head)
+        compiler_params=pltpu.CompilerParams(collective_id=0, has_side_effects=True, vmem_limit_bytes=50 * 1024 * 1024),
+    )(loss_scale, *(stay(a) for a in (lengths, pairs.T, pair_valid, attn, out_weight, resid, norm_gain, head)))
     g = misc[0:4].reshape(512)
     return (misc[4, 0:1], out, g * head.astype(F32), g * norm_gain.astype(F32))
 

time: 82.6 us -> 80.3 us (0.972)
  local copies, waits for them, and re-layouts: 3.46 us -> 1.49 us
    unnamed x5, local copies, waits for them, and re-layouts: 2.27 us -> 0.98 us
where the time goes in v5:
time: 80.3 us; the launch traced here: 79.3 us
  Pallas kernels  75.9 us (95%)
  local copies, waits for them, and re-layouts  1.49 us (2%)
  between operations  1.32 us (2%)
    pallas_call x1, Pallas kernels, shards(): pl.pallas_call(body, name='whole', out_shape=(jax.ShapeDtypeStruct((512,...  75.9 us

profile of v5, /device:TPU:4, one launch (start us, length us, event | category | flops | bytes accessed | tf_op | source)
XLA Modules:
  0.0 79.3 jit_solution(9745936522021647237)
XLA Ops:
  0.6 0.0 copy-start.1
  0.6 0.0 copy-start
  1.3 75.9 %whole.1 = (f32[512,512]{1,0:T(8,128)S(1)}, f32[8,128]{1,0:T(8,128)S(1)}) custom-call(f32[1]{0:T(128)S(6)} %copy.14.scale, s32[4]{0:T(128)} %lens_hbm.1, s32[2,4]{1,0:T(2,128)} %bitcast.5, s32[4]{0:T(128)} %valid_hbm.1, bf16[256,512]{1,0:T(8,128)(2,1)} %attn_hbm.1, bf16[8192,512]{1,0:T(8,128)(2,1)} %w_hbm.1, bf16[256,512]{1,0:T(8,128)(2,1)} %resid_hbm.1, ...), custom_call_target="tpu_custom_call" | custom-call | tf_op jit(solution)/shard_map/whole/pallas_call | solution.py:659
  77.2 0.5 slice.6
  77.7 0.0 copy-done.1
  77.7 0.0 copy-done
  77.7 0.6 bitcast_multiply_fusion
  78.3 1.0 %copy.15 = f32[512,512]{1,0:T(8,128)} copy(f32[512,512]{1,0:T(8,128)S(1)} %get-tuple-element.15) | data formatting | bytes 2097152
Async XLA Ops:
  0.6 77.1 %copy-start.1 = (bf16[512]{0:T(512)(128)(2,1)S(1)}, bf16[512]{0:T(512)(128)(2,1)}, u32[]{:S(2)}) copy-start(bf16[512]{0:T(512)(128)(2,1)} %head_hbm.1) | copy-start | bytes 3076
  0.6 77.1 %copy-start = (bf16[512]{0:T(512)(128)(2,1)S(1)}, bf16[512]{0:T(512)(128)(2,1)}, u32[]{:S(2)}) copy-start(bf16[512]{0:T(512)(128)(2,1)} %gain_hbm.1) | copy-start | bytes 3076

commit v6 on v5

--- a/solution.py
+++ b/solution.py
@@ -439,6 +439,9 @@
     row16 = lax.broadcasted_iota(jnp.int32, (16, 128), 0)
     pick = (lane16 & 15) == row16
     sa[r] = jnp.zeros((8, 128), F32)
+    ag2(0)
+    flip(1)
+    ag1(1)
     column = jnp.sum(acc[...], axis=1, keepdims=True)
     sa[r, 0:1, :] = jnp.sum(jnp.where(pick, column, 0.0), axis=0, keepdims=True)
     await_(dd.at[pl.ds(0, 15)], dd_rx)
@@ -457,9 +460,6 @@
 
     lax.fori_loop(1, 16, send_sa, 0)
     lax.fori_loop(0, 8, send_low, 0)
-    ag2(0)
-    flip(1)
-    ag1(1)
     ag3(0)
     await_(sa.at[pl.ds(0, 15)], sa_rx)
     sb[t] = jnp.zeros((8, 128), F32)
@@ -585,8 +585,8 @@
                     ag4part(1, 2)
 
             parts = []
-            for j in range(4):
-                tt = gi * 4 + j
+            for j in range(8):
+                tt = gi * 8 + j
                 k1 = kc[tt, 0:1, h * 128 : (h + 1) * 128]
                 c1 = kc[tt, 1:2, h * 128 : (h + 1) * 128]
                 for q in range(4):
@@ -610,7 +610,7 @@
                 out_ref[...] += prod
             return carry
 
-        lax.fori_loop(0, 4, group, 0)
+        lax.fori_loop(0, 2, group, 0)
 
     await_(att.at[pl.ds(0, 4), 0], att_rxc.at[0])
     await_(att.at[pl.ds(0, 4), 0], att_rxc.at[1])
@@ -672,7 +672,7 @@
             vm(little, BF16), vm(little, BF16), vm(little, BF16), vm(little, BF16), vm(little, BF16), vm(little, BF16),
             vm((2, 16, 4, 128, 128), BF16), vm((4, 128, 128), F32),
             vm((16, 8, 128), F32), vm((16, 8, 128), F32), vm((16, 256), F32), vm((16, 256), F32), vm((16, 8, 256), F32),
-            vm((8, 128), F32), vm((16, 8, 128), F32), vm((512, 512), BF16),
+            vm((8, 128), F32), vm((16, 8, 128), F32), vm((512, 1024), BF16),
             dma((2,)), dma((5,)), dma((8,)), dma, dma, dma((14,)), dma((2,)), dma, dma, dma((2,)), dma((2,)), dma, dma, dma, dma, dma, dma,
             dma((6,)), dma((6, 8)), dma, dma((2, 8)), dma, dma, dma, dma, dma, dma, dma, dma,
         ],

time: 80.3 us -> 77.8 us (0.969); the launches traced: 79.3 us -> 77.7 us
  Pallas kernels: 75.9 us -> 74.3 us
    pallas_call x1, Pallas kernels: 75.9 us -> 74.3 us  [shards(): pl.pallas_call(body, name='whole', out_shape=(jax.ShapeDtypeStruct((512,...]
where the time goes in v6:
time: 77.8 us; the launch traced here: 77.7 us
  Pallas kernels  74.3 us (96%)
  local copies, waits for them, and re-layouts  1.49 us (2%)
  between operations  1.32 us (2%)
    pallas_call x1, Pallas kernels, shards(): pl.pallas_call(body, name='whole', out_shape=(jax.ShapeDtypeStruct((512,...  74.3 us

profile of v6, /device:TPU:4, one launch (start us, length us, event | category | flops | bytes accessed | tf_op | source)
XLA Modules:
  0.0 77.7 jit_solution(4106950737556884021)
XLA Ops:
  0.6 0.0 copy-start.1
  0.6 0.0 copy-start
  1.3 74.3 %whole.1 = (f32[512,512]{1,0:T(8,128)S(1)}, f32[8,128]{1,0:T(8,128)S(1)}) custom-call(f32[1]{0:T(128)S(6)} %copy.14.scale, s32[4]{0:T(128)} %lens_hbm.1, s32[2,4]{1,0:T(2,128)} %bitcast.5, s32[4]{0:T(128)} %valid_hbm.1, bf16[256,512]{1,0:T(8,128)(2,1)} %attn_hbm.1, bf16[8192,512]{1,0:T(8,128)(2,1)} %w_hbm.1, bf16[256,512]{1,0:T(8,128)(2,1)} %resid_hbm.1, ...), custom_call_target="tpu_custom_call" | custom-call | tf_op jit(solution)/shard_map/whole/pallas_call | solution.py:659
  75.6 0.5 slice.6
  76.1 0.0 copy-done.1
  76.1 0.0 copy-done
  76.1 0.6 bitcast_multiply_fusion
  76.7 1.0 %copy.15 = f32[512,512]{1,0:T(8,128)} copy(f32[512,512]{1,0:T(8,128)S(1)} %get-tuple-element.15) | data formatting | bytes 2097152
Async XLA Ops:
  0.6 75.5 %copy-start.1 = (bf16[512]{0:T(512)(128)(2,1)S(1)}, bf16[512]{0:T(512)(128)(2,1)}, u32[]{:S(2)}) copy-start(bf16[512]{0:T(512)(128)(2,1)} %head_hbm.1) | copy-start | bytes 3076
  0.6 75.5 %copy-start = (bf16[512]{0:T(512)(128)(2,1)S(1)}, bf16[512]{0:T(512)(128)(2,1)}, u32[]{:S(2)}) copy-start(bf16[512]{0:T(512)(128)(2,1)} %gain_hbm.1) | copy-start | bytes 3076

commit v7 on v6

--- a/solution.py
+++ b/solution.py
@@ -340,6 +340,8 @@
         for g in quarters:
             gsend(h, g, "a0", "b0", "dan", 0)
             gsend(h, g, "a0", "b0", "dao", 1)
+
+    def ag1cross(h):
         for g in quarters:
             gsend(h, g, "a0", "b0", "dbn", 3)
             gsend(h, g, "a0", "b0", "dbo", 7)
@@ -421,6 +423,10 @@
         def _():
             flip(0)
             ag1(0)
+
+        @pl.when(n == 23)
+        def _():
+            ag1cross(0)
 
         return carry
 
@@ -442,6 +448,7 @@
     ag2(0)
     flip(1)
     ag1(1)
+    ag1cross(1)
     column = jnp.sum(acc[...], axis=1, keepdims=True)
     sa[r, 0:1, :] = jnp.sum(jnp.where(pick, column, 0.0), axis=0, keepdims=True)
     await_(dd.at[pl.ds(0, 15)], dd_rx)

time: 77.8 us -> 76.1 us (0.978)
  Pallas kernels: 74.3 us -> 72.6 us
    pallas_call x1, Pallas kernels: 74.3 us -> 72.6 us  [shards(): pl.pallas_call(body, name='whole', out_shape=(jax.ShapeDtypeStruct((512,...]
where the time goes in v7:
time: 76.1 us; the launch traced here: 76 us
  Pallas kernels  72.6 us (95%)
  local copies, waits for them, and re-layouts  1.49 us (2%)
  between operations  1.32 us (2%)
    pallas_call x1, Pallas kernels, shards(): pl.pallas_call(body, name='whole', out_shape=(jax.ShapeDtypeStruct((512,...  72.6 us

profile of v7, /device:TPU:4, one launch (start us, length us, event | category | flops | bytes accessed | tf_op | source)
XLA Modules:
  0.0 76.0 jit_solution(5269805450225036909)
XLA Ops:
  0.6 0.0 copy-start.1
  0.6 0.0 copy-start
  1.3 72.6 %whole.1 = (f32[512,512]{1,0:T(8,128)S(1)}, f32[8,128]{1,0:T(8,128)S(1)}) custom-call(f32[1]{0:T(128)S(6)} %copy.14.scale, s32[4]{0:T(128)} %lens_hbm.1, s32[2,4]{1,0:T(2,128)} %bitcast.5, s32[4]{0:T(128)} %valid_hbm.1, bf16[256,512]{1,0:T(8,128)(2,1)} %attn_hbm.1, bf16[8192,512]{1,0:T(8,128)(2,1)} %w_hbm.1, bf16[256,512]{1,0:T(8,128)(2,1)} %resid_hbm.1, ...), custom_call_target="tpu_custom_call" | custom-call | tf_op jit(solution)/shard_map/whole/pallas_call | solution.py:666
  74.0 0.5 slice.6
  74.5 0.0 copy-done.1
  74.5 0.0 copy-done
  74.5 0.6 bitcast_multiply_fusion
  75.1 1.0 %copy.15 = f32[512,512]{1,0:T(8,128)} copy(f32[512,512]{1,0:T(8,128)S(1)} %get-tuple-element.15) | data formatting | bytes 2097152
Async XLA Ops:
  0.6 73.8 %copy-start.1 = (bf16[512]{0:T(512)(128)(2,1)S(1)}, bf16[512]{0:T(512)(128)(2,1)}, u32[]{:S(2)}) copy-start(bf16[512]{0:T(512)(128)(2,1)} %head_hbm.1) | copy-start | bytes 3076
  0.6 73.8 %copy-start = (bf16[512]{0:T(512)(128)(2,1)S(1)}, bf16[512]{0:T(512)(128)(2,1)}, u32[]{:S(2)}) copy-start(bf16[512]{0:T(512)(128)(2,1)} %gain_hbm.1) | copy-start | bytes 3076
